TPU v7x, 32 devices: a whole 2x2x4 slice. The times are simulated.
32 devices in a mesh: dp: 2 (over x), etp: 4 (over z), ep: 4 (over y, core).
Axes of the slice: x: 2, y: 2, z: 4, core: 2. Of those that a mesh axis runs over, the one named last changes fastest.
Arguments:
- u_rows: bfloat16 [6144, 1536], P(('dp', 'ep', 'etp')), parts along dimension 0
- dy_rows: bfloat16 [6144, 1536], P(('dp', 'ep', 'etp')), parts along dimension 0
- topk_ids: int32 [6144, 4], P(('dp', 'ep', 'etp')), parts along dimension 0
- w_router: bfloat16 [1536, 32], replicated
- w_gate: bfloat16 [32, 1536, 768], P('ep', None, 'etp')
- w_up: bfloat16 [32, 1536, 768], P('ep', None, 'etp')
- w_down: bfloat16 [32, 768, 1536], P('ep', 'etp')
Outputs:
- output 1: bfloat16 [6144, 1536], P(('dp', 'ep', 'etp')), parts along dimension 0
- output 2: bfloat16 [6144, 1536], P(('dp', 'ep', 'etp')), parts along dimension 0
- output 3: float32 [64, 1536, 768], P(('dp', 'ep'), None, 'etp'), parts along dimension 0
- output 4: float32 [64, 1536, 768], P(('dp', 'ep'), None, 'etp'), parts along dimension 0
- output 5: float32 [64, 768, 1536], P(('dp', 'ep'), 'etp'), parts along dimension 0
- output 6: float32 [3072, 32], P('dp'), parts along dimension 0
There are 2 independent parts. A program takes and returns all parts, laid end to end along the dimension named above; an argument that names none is the same for every part.
All inputs are finite; a program needn't handle non-finite values.
Results may differ from a plain program's by a relative error of at most 0.0112347.
Values are sent between devices in bfloat16 or wider.
A program may use at most 1 GiB of HBM per device.

v0:
```python
import jax
import jax.numpy as jnp
from jax import lax
from jax.sharding import PartitionSpec as P


def row_bound(tok_dev, top_k, experts):
    return min(tok_dev, (4 * tok_dev * top_k + experts - 1) // experts)


def slot_layout(expert_ids, experts, slot_count):
    tokens, top_k = expert_ids.shape
    flat_ids = expert_ids.reshape(-1)
    one_hot = (flat_ids[:, None] == jnp.arange(experts, dtype=jnp.int32)[None, :]).astype(jnp.int32)
    pair_rank = jnp.sum((jnp.cumsum(one_hot, axis=0) - one_hot) * one_hot, axis=1)
    pair_slot = flat_ids * slot_count + pair_rank
    slot_pair = jnp.full((experts * slot_count,), tokens * top_k, jnp.int32).at[pair_slot].set(jnp.arange(tokens * top_k, dtype=jnp.int32))
    return pair_slot.reshape(tokens, top_k), slot_pair


def solution(mesh):
    ep_size = mesh.shape["ep"]
    etp_size = mesh.shape["etp"]
    tok_spec = P(("dp", "ep", "etp"), None)
    col_spec = P("ep", None, "etp")
    row_spec = P("ep", "etp", None)
    in_specs = (tok_spec, tok_spec, tok_spec, P(None, None), col_spec, col_spec, row_spec)
    out_specs = (tok_spec, tok_spec, P(("dp", "ep"), None, "etp"), P(("dp", "ep"), None, "etp"), P(("dp", "ep"), "etp", None), P("dp", None))

    def device_step(u_loc, dy_loc, ids_loc, w_router, w_gate, w_up, w_down):
        tok_dev, d_model = u_loc.shape
        top_k = ids_loc.shape[1]
        experts = w_router.shape[1]
        local_exp = w_gate.shape[0]
        cap_slots = etp_size * row_bound(tok_dev, top_k, experts)
        logits = jnp.dot(u_loc, w_router, preferred_element_type=jnp.float32)
        router_prob = jax.nn.softmax(logits, axis=-1)
        gate_loc = jnp.take_along_axis(router_prob, ids_loc, axis=1)
        u_grp = lax.all_gather(u_loc, "etp", axis=0, tiled=True)
        ids_grp = lax.all_gather(ids_loc, "etp", axis=0, tiled=True)
        gate_grp = lax.all_gather(gate_loc, "etp", axis=0, tiled=True)
        pair_slot, slot_pair = slot_layout(ids_grp, experts, cap_slots)
        slot_tok = slot_pair // top_k
        x_send = jnp.take(u_grp, slot_tok, axis=0, mode="fill", fill_value=0)
        x_recv = lax.all_to_all(x_send.reshape(experts, cap_slots, d_model), "ep", 0, 0, tiled=True).reshape(ep_size, local_exp, cap_slots, d_model)
        h_gate = jnp.einsum("secd,edf->secf", x_recv, w_gate, preferred_element_type=jnp.float32).astype(jnp.bfloat16)
        h_up = jnp.einsum("secd,edf->secf", x_recv, w_up, preferred_element_type=jnp.float32).astype(jnp.bfloat16)
        gate_f32 = h_gate.astype(jnp.float32)
        up_f32 = h_up.astype(jnp.float32)
        sig_gate = jax.nn.sigmoid(gate_f32)
        silu_gate = gate_f32 * sig_gate
        act_rows = (silu_gate * up_f32).astype(jnp.bfloat16)
        out_part = jnp.einsum("secf,efd->secd", act_rows, w_down, preferred_element_type=jnp.float32).astype(jnp.bfloat16)
        out_back = lax.all_to_all(out_part.reshape(experts, cap_slots, d_model), "ep", 0, 0, tiled=True)
        out_pairs = jnp.take(out_back.reshape(experts * cap_slots, d_model), pair_slot, axis=0)
        moe_part = jnp.einsum("tk,tkd->td", gate_grp, out_pairs, preferred_element_type=jnp.float32)
        moe_own = lax.psum_scatter(moe_part, "etp", scatter_dimension=0, tiled=True)
        y_loc = (u_loc.astype(jnp.float32) + moe_own).astype(jnp.bfloat16)

        dy_grp = lax.all_gather(dy_loc, "etp", axis=0, tiled=True)
        dgate_part = jnp.einsum("td,tkd->tk", dy_grp, out_pairs, preferred_element_type=jnp.float32)
        dgate_loc = lax.psum_scatter(dgate_part, "etp", scatter_dimension=0, tiled=True)
        slot_gate = jnp.take(gate_grp.reshape(-1), slot_pair, mode="fill", fill_value=0.0)
        cot_slots = jnp.take(dy_grp, slot_tok, axis=0, mode="fill", fill_value=0)
        do_send = (cot_slots.astype(jnp.float32) * slot_gate[:, None]).astype(jnp.bfloat16)
        do_recv = lax.all_to_all(do_send.reshape(experts, cap_slots, d_model), "ep", 0, 0, tiled=True).reshape(ep_size, local_exp, cap_slots, d_model)
        dw_down = jnp.einsum("secf,secd->efd", act_rows, do_recv, preferred_element_type=jnp.float32)
        d_act = jnp.einsum("secd,efd->secf", do_recv, w_down, preferred_element_type=jnp.float32).astype(jnp.bfloat16).astype(jnp.float32)
        d_gate_h = (d_act * up_f32 * sig_gate * (1.0 + gate_f32 * (1.0 - sig_gate))).astype(jnp.bfloat16)
        d_up_h = (d_act * silu_gate).astype(jnp.bfloat16)
        dw_gate = jnp.einsum("secd,secf->edf", x_recv, d_gate_h, preferred_element_type=jnp.float32)
        dw_up = jnp.einsum("secd,secf->edf", x_recv, d_up_h, preferred_element_type=jnp.float32)
        dx_part = (jnp.einsum("secf,edf->secd", d_gate_h, w_gate, preferred_element_type=jnp.float32) + jnp.einsum("secf,edf->secd", d_up_h, w_up, preferred_element_type=jnp.float32)).astype(jnp.bfloat16)
        dx_back = lax.all_to_all(dx_part.reshape(experts, cap_slots, d_model), "ep", 0, 0, tiled=True)
        dx_pairs = jnp.take(dx_back.reshape(experts * cap_slots, d_model), pair_slot, axis=0)
        du_part = jnp.sum(dx_pairs, axis=1, dtype=jnp.float32)
        du_moe = lax.psum_scatter(du_part, "etp", scatter_dimension=0, tiled=True)
        expert_hot = (ids_loc[:, :, None] == jnp.arange(experts, dtype=jnp.int32)[None, None, :]).astype(jnp.float32)
        d_prob = jnp.einsum("tk,tke->te", dgate_loc, expert_hot)
        d_logit = router_prob * (d_prob - jnp.sum(router_prob * d_prob, axis=-1, keepdims=True))
        dw_router = lax.psum(jnp.einsum("td,te->de", u_loc, d_logit, preferred_element_type=jnp.float32), ("etp", "ep"))
        du_router = jnp.einsum("te,de->td", d_logit, w_router, preferred_element_type=jnp.float32)
        du_loc = (dy_loc.astype(jnp.float32) + du_moe + du_router).astype(jnp.bfloat16)
        return y_loc, du_loc, dw_gate, dw_up, dw_down, dw_router

    return jax.shard_map(device_step, mesh=mesh, in_specs=in_specs, out_specs=out_specs, check_vma=False)
```

profile of v0, /device:TPU:0, one launch (start us, length us, event | category | flops | bytes accessed | tf_op | source)
XLA Modules:
  0.0 2618.8 jit_solution(10667265227914876918)
XLA Ops:
  7.9 14.8 all-gather.1
  34.9 11.8 scatter_custom_fusion
  47.5 14.5 all-gather.5.cloned.1.call-done
  62.0 75.5 %gather_fusion.2 = bf16[12288,1536]{1,0:T(8,128)(2,1)} fusion(bf16[768,1536]{1,0:T(8,128)(2,1)} %all-gather.5.cloned.1.call-done, s32[12288]{0:T(1024)S(1)} %get-tuple-element.15), kind=kCustom, calls=%fused_computation.clone | custom fusion | bytes 75546624 | tf_op jit(solution)/shard_map/jit(_take)/gather | solution.py:44
  137.5 25.5 broadcast_select_fusion
  163.0 427.7 %all_to_all.20 = bf16[32,384,1536]{2,1,0:T(8,128)(2,1)} all-to-all(bf16[32,384,1536]{2,1,0:T(8,128)(2,1)} %bitcast.158), channel_id=1, replica_groups=mesh['dp'=2,'etp'=4,'ep'=4] {'ep'}, dimensions={0} | all-to-all | bytes 75497472 | tf_op jit(solution)/shard_map/all_to_all | solution.py:45
  590.6 19.8 fusion.40
  610.4 18.7 fusion.35
  629.1 19.7 convert_bitcast_fusion
  648.8 26.0 copy.81
  688.2 404.9 %all-to-all-done.1 = bf16[32,384,1536]{2,1,0:T(8,128)(2,1)} async-done(((bf16[32,384,1536]{2,1,0:T(8,128)(2,1)}), bf16[32,384,1536]{2,1,0:T(8,128)(2,1)}, u32[]{:S(2)}, u32[]{:S(2)}) %all-to-all-start.1) | async-done | bytes 37748768 | tf_op jit(solution)/shard_map/all_to_all | solution.py:54
  1093.0 65.7 %gather_fusion.3 = bf16[3072,1536]{1,0:T(8,128)(2,1)} fusion(bf16[12288,1536]{1,0:T(8,128)(2,1)} %bitcast.21, s32[3072]{0:T(1024)S(1)} %broadcast_clamp_fusion.1), kind=kCustom, calls=%fused_computation.1.clone | custom fusion | bytes 18886656 | tf_op jit(solution)/shard_map/jit(_take)/gather | solution.py:55
  1158.8 16.0 reshape.209
  1174.8 17.3 fusion.18
  1192.6 55.8 %gather_fusion.4 = bf16[12288,1536]{1,0:T(8,128)(2,1)} fusion(bf16[768,1536]{1,0:T(8,128)(2,1)S(1)} %copy-done.3, s32[12288]{0:T(1024)S(1)} %copy-done.16), kind=kCustom, calls=%fused_computation.2.clone | custom fusion | bytes 75546624 | tf_op jit(solution)/shard_map/jit(_take)/gather | solution.py:64
  1257.0 13.1 all-gather
  1270.5 68.0 %gather_fusion = f32[12288]{0:T(1024)S(1)} fusion(f32[3072]{0:T(1024)S(1)} %reshape.123, s32[12288]{0:T(1024)S(1)} %copy-done.19), kind=kCustom, calls=%fused_computation.4 | custom fusion | bytes 147456 | tf_op jit(solution)/shard_map/jit(_take)/gather | solution.py:63
  1338.6 25.8 multiply_convert_fusion
  1364.3 427.5 %all_to_all.21 = bf16[32,384,1536]{2,1,0:T(8,128)(2,1)} all-to-all(bf16[32,384,1536]{2,1,0:T(8,128)(2,1)} %bitcast.161), channel_id=1, replica_groups=mesh['dp'=2,'etp'=4,'ep'=4] {'ep'}, dimensions={0} | all-to-all | bytes 75497472 | tf_op jit(solution)/shard_map/all_to_all | solution.py:66
  1791.9 23.2 fusion.12
  1815.1 30.3 %fusion.25 = f32[8,4,384,1536]{3,2,1,0:T(8,128)} fusion(bf16[4,8,384,192]{2,3,0,1:T(8,128)(2,1)} %get-tuple-element.13, bf16[8,1536,192]{1,2,0:T(8,128)(2,1)} %param.15), kind=kOutput, calls=%fused_computation.44 | convolution fusion | flops 7247757312 | bytes 84934656 | tf_op jit(solution)/shard_map/secf,edf->secd/dot_general | solution.py:73
  1845.4 40.7 %fusion = bf16[4,8,384,1536]{3,2,0,1:T(8,128)(2,1)} fusion(f32[8,4,384,1536]{3,2,1,0:T(8,128)} %fusion.25, bf16[4,8,384,192]{2,3,0,1:T(8,128)(2,1)} %get-tuple-element.12, bf16[8,1536,192]{1,2,0:T(8,128)(2,1)} %param.16), kind=kOutput, calls=%fused_computation.9 | convolution fusion | flops 7285506048 | bytes 122683392 | tf_op jit(solution)/shard_map/secf,edf->secd/dot_general | solution.py:73
  1886.1 25.9 copy.86
  1933.3 396.8 %all-to-all-done.3 = bf16[32,384,1536]{2,1,0:T(8,128)(2,1)} async-done(((bf16[32,384,1536]{2,1,0:T(8,128)(2,1)}), bf16[32,384,1536]{2,1,0:T(8,128)(2,1)}, u32[]{:S(2)}, u32[]{:S(2)}) %all-to-all-start.3) | async-done | bytes 37748768 | tf_op jit(solution)/shard_map/all_to_all | solution.py:74
  2330.1 65.7 %gather_fusion.5 = bf16[3072,1536]{1,0:T(8,128)(2,1)} fusion(bf16[12288,1536]{1,0:T(8,128)(2,1)} %bitcast.31, s32[3072]{0:T(1024)S(1)} %copy-done.5), kind=kCustom, calls=%fused_computation.3.clone | custom fusion | bytes 18886656 | tf_op jit(solution)/shard_map/jit(_take)/gather | solution.py:75
  2395.8 16.0 reshape.215
  2411.9 19.6 convert_reduce_fusion
  2434.7 20.6 fusion.20
  2455.3 20.0 convolution_bitcast_fusion
  2475.3 20.1 convolution_bitcast_fusion.1
  2495.4 19.4 reduce-scatter.6.cloned.1.call-done
  2517.3 92.6 %all-reduce.2.cloned.1.call-done = f32[1536,32]{0,1:T(8,128)} async-done(((f32[1536,32]{0,1:T(8,128)}), f32[1536,32]{0,1:T(8,128)}) %all-reduce.2.cloned.1.call-update) | async-done | bytes 196624 | tf_op jit(solution)/shard_map/psum | solution.py:81
  (126 shorter events, 64.8 us)
Async XLA Ops:
  7.2 680.7 %copy-start = (bf16[1536,32]{0,1:T(8,128)(2,1)S(1)}, bf16[1536,32]{0,1:T(8,128)(2,1)}, u32[]{:S(2)}) copy-start(bf16[1536,32]{0,1:T(8,128)(2,1)} %param.14) | copy-start | bytes 294916
  7.2 54.8 %all-gather.5.cloned.1.call-start = ((), (), s32[]{:S(2)}) async-start(), calls=%async_computation.7 | async-start | bytes 2949120 | tf_op jit(solution)/shard_map/all_gather | solution.py:39
  46.7 90.7 %copy-start.11 = (s32[12288]{0:T(1024)}, s32[12288]{0:T(1024)S(1)}, u32[]{:S(2)}) copy-start(s32[12288]{0:T(1024)S(1)} %scatter_custom_fusion) | copy-start | bytes 147460
  46.8 90.6 %copy-start.24 = (pred[12288]{0:T(1024)(128)(4,1)}, pred[12288]{0:T(1024)(128)(4,1)S(1)}, u32[]{:S(2)}) copy-start(pred[12288]{0:T(1024)(128)(4,1)S(1)} %compare_and_fusion) | copy-start | bytes 36868
  47.5 90.0 %copy-start.15 = (s32[12288]{0:T(1024)}, s32[12288]{0:T(1024)S(1)}, u32[]{:S(2)}) copy-start(s32[12288]{0:T(1024)S(1)} %get-tuple-element.15) | copy-start | bytes 147460
  137.5 472.9 %slice-start = ((s8[4718592]{0:T(1024)(128)(4,1)}), s8[524288]{0:T(1024)(128)(4,1)S(1)}, s32[]{:S(2)}) async-start(s8[4718592]{0:T(1024)(128)(4,1)} %bitcast.165), calls=%async_computation.13 | async-start | bytes 1048576
  163.0 447.4 %slice-start.1 = ((s8[4718592]{0:T(1024)(128)(4,1)}), s8[4194304]{0:T(1024)(128)(4,1)S(1)}, s32[]{:S(2)}) async-start(s8[4718592]{0:T(1024)(128)(4,1)} %bitcast.165), calls=%async_computation.14 | async-start | bytes 8388608
  674.8 11.7 copy-start.21
  674.8 11.7 copy-start.23
  674.8 13.0 copy-start.26
  674.8 13.1 copy-start.6
  674.8 418.2 %all-to-all-start.1 = ((bf16[32,384,1536]{2,1,0:T(8,128)(2,1)}), bf16[32,384,1536]{2,1,0:T(8,128)(2,1)}, u32[]{:S(2)}, u32[]{:S(2)}) async-start(bf16[32,384,1536]{2,1,0:T(8,128)(2,1)} %bitcast.159), calls=%async_computation.1 | async-start | bytes 75497472 | tf_op jit(solution)/shard_map/all_to_all | solution.py:54
  685.6 489.2 %all-gather.7.cloned.1.call-start = ((), (), s32[]{:S(2)}) async-start(), calls=%async_computation.9 | async-start | bytes 2949120 | tf_op jit(solution)/shard_map/all_gather | solution.py:60
  686.4 562.0 %reduce-scatter.8.cloned.1.call-start = ((), (), s32[]{:S(2)}) async-start(), calls=%async_computation.11 | async-start | bytes 491520 | tf_op jit(solution)/shard_map/reduce_scatter | solution.py:62
  687.4 487.5 %copy-start.17 = (pred[768,4]{1,0:T(8,128)(4,1)}, pred[768,4]{1,0:T(8,128)(4,1)S(1)}, u32[]{:S(2)}) copy-start(pred[768,4]{1,0:T(8,128)(4,1)S(1)} %copy.77) | copy-start | bytes 9220
  687.8 470.9 %copy-start.4 = (s32[3072]{0:T(1024)}, s32[3072]{0:T(1024)S(1)}, u32[]{:S(2)}) copy-start(s32[3072]{0:T(1024)S(1)} %broadcast_clamp_fusion.1) | copy-start | bytes 36868
  1174.8 17.8 copy-start.3
  1174.8 17.8 copy-start.16
  1250.4 20.0 copy-start.19
  1270.2 68.3 %copy-start.9 = (f32[4,192,4]{2,1,0:T(8,128)}, f32[4,192,4]{2,1,0:T(8,128)S(1)}, u32[]{:S(2)}) copy-start(f32[4,192,4]{2,1,0:T(8,128)S(1)} %copy.102) | copy-start | bytes 36868
  1270.4 68.1 %copy-start.12 = (s32[12288]{0:T(1024)S(1)}, s32[12288]{0:T(1024)}, u32[]{:S(2)}) copy-start(s32[12288]{0:T(1024)} %copy-done.11) | copy-start | bytes 147460
  1270.5 68.1 %copy-start.25 = (pred[12288]{0:T(1024)(128)(4,1)S(1)}, pred[12288]{0:T(1024)(128)(4,1)}, u32[]{:S(2)}) copy-start(pred[12288]{0:T(1024)(128)(4,1)} %copy-done.24) | copy-start | bytes 36868
  1912.0 418.1 %all-to-all-start.3 = ((bf16[32,384,1536]{2,1,0:T(8,128)(2,1)}), bf16[32,384,1536]{2,1,0:T(8,128)(2,1)}, u32[]{:S(2)}, u32[]{:S(2)}) async-start(bf16[32,384,1536]{2,1,0:T(8,128)(2,1)} %bitcast.160), calls=%async_computation.4 | async-start | bytes 75497472 | tf_op jit(solution)/shard_map/all_to_all | solution.py:74
  1922.7 509.9 %reduce-scatter.4.cloned.1.call-start = ((), (), s32[]{:S(2)}) async-start(), calls=%async_computation.8 | async-start | bytes 5898240 | tf_op jit(solution)/shard_map/reduce_scatter | solution.py:57
  1930.4 399.7 %copy-start.5 = (s32[3072]{0:T(1024)S(1)}, s32[3072]{0:T(1024)}, u32[]{:S(2)}) copy-start(s32[3072]{0:T(1024)} %copy-done.4) | copy-start | bytes 36868
  1933.0 581.8 %reduce-scatter.6.cloned.1.call-start = ((), (), s32[]{:S(2)}) async-start(), calls=%async_computation.10 | async-start | bytes 5898240 | tf_op jit(solution)/shard_map/reduce_scatter | solution.py:77
  2411.9 19.7 copy-start.2
  2411.9 19.7 copy-start.7
  2411.9 19.7 copy-start.14
  2411.9 19.7 copy-start.27
  2431.5 178.4 %all-reduce.2.cloned.1.call-start = ((), (), s32[]{:S(2)}) async-start(), calls=%async_computation.12 | async-start | bytes 393216 | tf_op jit(solution)/shard_map/psum | solution.py:81
  2475.3 39.5 %copy-start.8 = (bf16[192,1536]{1,0:T(8,128)(2,1)S(1)}, bf16[192,1536]{1,0:T(8,128)(2,1)}, u32[]{:S(2)}) copy-start(bf16[192,1536]{1,0:T(8,128)(2,1)} %param.12) | copy-start | bytes 1769476
  (6 other events, 29.7 us)
Sparse Core Ops, SparseCore 0:
  9.6 52.3 all-gather.4
  688.0 49.0 all-gather.6
  1192.3 18.8 reduce-scatter.7
  1933.1 84.5 reduce-scatter.3
  2431.6 83.1 reduce-scatter.5
  2518.7 91.1 all-reduce.1
where the time goes:
time: 2630 us; the launch traced here: 2620 us
  waiting for transfers between devices  930 us (35%)
  blocking collectives  883 us (34%)
  local copies, waits for them, and re-layouts  442 us (17%)
  matrix products  243 us (9%)
  other arithmetic  84.2 us (3%)
    all_to_all x1, blocking collectives, device_step(): lax.all_to_all(x_send.reshape(experts, cap_slots, d_model), 'ep', 0, 0, t...  428 us
    all_to_all x1, blocking collectives, device_step(): lax.all_to_all(do_send.reshape(experts, cap_slots, d_model), 'ep', 0, 0,...  428 us
    all_to_all x1, waiting for transfers between devices, device_step(): lax.all_to_all(out_part.reshape(experts, cap_slots, d_model), 'ep', 0, 0,...  405 us
    all_to_all x1, waiting for transfers between devices, device_step(): lax.all_to_all(dx_part.reshape(experts, cap_slots, d_model), 'ep', 0, 0,...  397 us
    psum x1, waiting for transfers between devices, device_step(): lax.psum(jnp.einsum('td,te->de', u_loc, d_logit, preferred_element_type=j...  92.6 us
    gather x2, local copies, waits for them, and re-layouts, device_step(): jnp.take(out_back.reshape(experts * cap_slots, d_model), pair_slot, axis=0)  81.8 us
    gather x2, local copies, waits for them, and re-layouts, device_step(): jnp.take(dx_back.reshape(experts * cap_slots, d_model), pair_slot, axis=0)  81.8 us
    gather x1, local copies, waits for them, and re-layouts, device_step(): x_send = jnp.take(u_grp, slot_tok, axis=0, mode='fill', fill_value=0)  75.5 us
  transfers between devices with their start and end apart: 8, of which 5 were waited for; matrix products, arithmetic and copies ran while one was open for 13% of the time, Pallas kernels for 0%

commit v1 on v0

v1 whole, which is shorter than its diff:
```python
import jax
import jax.numpy as jnp
from jax import lax
from jax.experimental import pallas as pl
from jax.experimental.pallas import tpu as pltpu
from jax.sharding import PartitionSpec as P

MESH = pl.DeviceIdType.MESH
F32 = jnp.float32
BF16 = jnp.bfloat16
LANES = 256
LEVEL_ROWS = 32
HALF = 8
CHUNK = 512


def dot_nn(a, b):
    return lax.dot_general(a, b, (((1,), (0,)), ((), ())), preferred_element_type=F32)


def dot_nt(a, b):
    return lax.dot_general(a, b, (((1,), (1,)), ((), ())), preferred_element_type=F32)


def dot_tn(a, b):
    return lax.dot_general(a, b, (((0,), (0,)), ((), ())), preferred_element_type=F32)


def position():
    ep = lax.axis_index("ep")
    z = lax.axis_index("etp")
    return ep // 2, ep % 2, z


def block_of(y, c, z):
    return (y * 2 + c) * 4 + z


def near_order(z, q):
    near = z - 1 + 2 * (1 - jnp.minimum(z, 1))
    far = 3 * (1 - z // 2)
    third = 6 - z - near - far
    return jnp.where(q == 0, z, jnp.where(q == 1, near, jnp.where(q == 2, third, far)))


def far_order(z, k):
    first = 3 * (1 - z // 2)
    second = (2 + 3 * z) % 5
    third = 1 + z % 2
    return jnp.where(k == 0, first, jnp.where(k == 1, second, jnp.where(k == 2, third, z)))


def one_hot_slots(rank, cap):
    tok = rank.shape[1]
    experts = rank.shape[0]
    row = lax.broadcasted_iota(jnp.int32, (experts, cap, tok), 1).astype(F32)
    hit = rank[:, None, :] == row
    return jnp.where(hit, 1.0, 0.0).reshape(experts * cap, tok).astype(BF16)


def split3(x):
    hi = x.astype(BF16)
    rest = x - hi.astype(F32)
    mid = rest.astype(BF16)
    low = (rest - mid.astype(F32)).astype(BF16)
    return jnp.concatenate([hi, mid, low], axis=0)


def gather_kernel(u_ref, dy_ref, ids_ref, wr_ref, x_ref, d_ref, uall_ref, rank_ref, g_ref, prob_ref, gown_ref,
                  rcv, pbuf, xbuf, in_sem, send_sem, recv_sem, meta_send, meta_recv, out_sem, uout_sem):
    y, c, z = position()
    me = block_of(y, c, z)
    tok = u_ref.shape[0]
    d_model = u_ref.shape[1]
    experts = wr_ref.shape[0]
    local = rank_ref.shape[1]
    cap = pbuf.shape[0] // local
    blocks = rcv.shape[1]

    own_u = pltpu.make_async_copy(u_ref, rcv.at[0, me], in_sem.at[0])
    own_d = pltpu.make_async_copy(dy_ref, rcv.at[1, me], in_sem.at[1])
    own_u.start()
    own_d.start()

    def rdma(arr, s, kind, ep_to, z_to):
        return pltpu.make_async_remote_copy(
            src_ref=rcv.at[arr, s], dst_ref=rcv.at[arr, s], send_sem=send_sem.at[arr, s, kind],
            recv_sem=recv_sem.at[arr, s], device_id={"ep": ep_to, "etp": z_to}, device_id_type=MESH)

    ep_sib = y * 2 + 1 - c
    ep_y = (1 - y) * 2 + c
    ep_me = y * 2 + c

    def send_down(arr, s):
        return rdma(arr, s, 0, ep_me, jnp.maximum(z - 1, 0))

    def send_up(arr, s):
        return rdma(arr, s, 1, ep_me, jnp.minimum(z + 1, 3))

    def send_y(arr, s):
        return rdma(arr, s, 2, ep_y, z)

    def send_sib(arr, s):
        return rdma(arr, s, 3, ep_sib, z)

    for arr, own in ((0, own_u), (1, own_d)):
        own.wait()

        @pl.when(z > 0)
        def _():
            send_down(arr, me).start()

        @pl.when(z < 3)
        def _():
            send_up(arr, me).start()

        send_y(arr, me).start()
        send_sib(arr, me).start()

    logits = dot_nt(wr_ref[...], rcv[0, me])
    shifted = jnp.exp(logits - jnp.max(logits, axis=0, keepdims=True))
    prob = shifted / jnp.sum(shifted, axis=0, keepdims=True)
    expert_row = lax.broadcasted_iota(jnp.int32, (experts, tok), 0)
    chosen = expert_row == ids_ref[0:1, :]
    for j in range(1, ids_ref.shape[0]):
        chosen = chosen | (expert_row == ids_ref[j:j + 1, :])
    prob_ref[...] = jnp.zeros(prob_ref.shape, F32)
    prob_ref[:, 0:tok] = prob
    gown_ref[...] = jnp.full(gown_ref.shape, -1.0, F32)
    gown_ref[:, 0:tok] = jnp.where(chosen, prob, -1.0)
    g_ref[me] = gown_ref[pl.ds(pl.multiple_of(ep_me * local, local), local), :]

    def meta_copy(s):
        ep_to = s // 4
        return pltpu.make_async_remote_copy(
            src_ref=gown_ref.at[pl.ds(pl.multiple_of(ep_to * local, local), local), :], dst_ref=g_ref.at[me],
            send_sem=meta_send.at[s], recv_sem=meta_recv.at[me], device_id={"ep": ep_to, "etp": s % 4},
            device_id_type=MESH)

    def meta_wait(s):
        return pltpu.make_async_remote_copy(
            src_ref=gown_ref.at[pl.ds(0, local), :], dst_ref=g_ref.at[s], send_sem=meta_send.at[s],
            recv_sem=meta_recv.at[s], device_id={"ep": ep_me, "etp": z}, device_id_type=MESH)

    @pl.loop(1, blocks)
    def _(i):
        meta_copy((me + i) % blocks).start()

    lower = (lax.broadcasted_iota(jnp.int32, (LANES, LANES), 0) < lax.broadcasted_iota(jnp.int32, (LANES, LANES), 1))
    before = jnp.where(lower, 1.0, 0.0).astype(BF16)

    def out_copy(arr_is_dy, slot, s):
        return pltpu.make_async_copy(xbuf.at[slot], (d_ref if arr_is_dy else x_ref).at[s], out_sem.at[slot])

    def u_copy(s):
        return pltpu.make_async_copy(rcv.at[0, s], uall_ref.at[s], uout_sem.at[s])

    @pl.loop(0, 5)
    def _(t):
        for arr in (0, 1):
            @pl.when((t >= 1) & (t <= 3))
            def _():
                zb = near_order(z, t)
                s = block_of(y, c, zb)
                send_y(arr, s).wait_recv()

                @pl.when((zb < z) & (z < 3))
                def _():
                    send_up(arr, s).start()

                @pl.when((zb > z) & (z > 0))
                def _():
                    send_down(arr, s).start()

                send_y(arr, s).start()
                send_sib(arr, s).start()

        for arr in (0, 1):
            @pl.when(t >= 1)
            def _():
                s = block_of(1 - y, c, near_order(z, t - 1))
                send_y(arr, s).wait_recv()
                send_sib(arr, s).start()

        lo = 4 * (t // 4)
        hi = jnp.where(t == 0, 4, 8)

        @pl.loop(lo, hi)
        def _(i):
            typ = i // 4
            arr = (i // 2) % 2
            flip = i % 2
            core = c + flip - 2 * c * flip
            zb = near_order(z, t - typ)
            yb = y + typ - 2 * y * typ
            s = block_of(yb, core, zb)
            j = jnp.maximum(8 * t - 4, 0) + i - lo
            slot = j % 2

            @pl.when(flip == 1)
            def _():
                send_y(arr, s).wait_recv()

            @pl.when(arr == 0)
            def _():
                u_copy(s).start()

                @pl.when(s != me)
                def _():
                    meta_wait(s).wait_recv()

                mask = g_ref[s] >= 0.0
                rank = dot_nn(jnp.where(mask, 1.0, 0.0).astype(BF16), before)
                rank_ref[s] = jnp.where(mask, rank, -1.0)

            pbuf[...] = one_hot_slots(rank_ref[s][:, 0:tok], cap)

            @pl.when(j >= 2)
            def _():
                out_copy(False, slot, s).wait()

            @pl.loop(0, d_model // CHUNK)
            def _(n):
                cols = pl.ds(pl.multiple_of(n * CHUNK, CHUNK), CHUNK)
                xbuf[slot, :, cols] = dot_nn(pbuf[...], rcv[arr, s, :, cols]).astype(BF16)

            @pl.when(arr == 0)
            def _():
                out_copy(False, slot, s).start()

            @pl.when(arr == 1)
            def _():
                out_copy(True, slot, s).start()

    for slot in (0, 1):
        out_copy(False, slot, me).wait()

    @pl.loop(0, blocks)
    def _(s):
        u_copy(s).wait()

        @pl.when(s != me)
        def _():
            meta_copy(s).wait_send()

    @pl.loop(0, 4)
    def _(q):
        zb = near_order(z, q)
        s = block_of(y, c, zb)
        sy = block_of(1 - y, c, zb)
        for arr in (0, 1):
            @pl.when((z > 0) & (zb >= z))
            def _():
                send_down(arr, s).wait_send()

            @pl.when((z < 3) & (zb <= z))
            def _():
                send_up(arr, s).wait_send()

            send_y(arr, s).wait_send()
            send_sib(arr, s).wait_send()
            send_sib(arr, sy).wait_send()


def expert_kernel(te, tl, th, count, x_ref, d_ref, wg_ref, wu_ref, wd_ref, rank_ref, g_ref,
                  go_ref, dx_ref, dwg_ref, dwu_ref, dwd_ref, dg_ref):
    i = pl.program_id(0)

    @pl.when(i < count[0])
    def _():
        expert_tile(i, te, tl, th, x_ref, d_ref, wg_ref, wu_ref, wd_ref, rank_ref, g_ref, go_ref, dx_ref, dwg_ref, dwu_ref, dwd_ref, dg_ref)


def expert_tile(i, te, tl, th, x_ref, d_ref, wg_ref, wu_ref, wd_ref, rank_ref, g_ref,
                go_ref, dx_ref, dwg_ref, dwu_ref, dwd_ref, dg_ref):
    e = te[i]
    level = tl[i]
    half = th[i]
    rows = HALF * LEVEL_ROWS
    d_model = x_ref.shape[-1]
    fresh = (i == 0) | (te[jnp.maximum(i - 1, 0)] != e)

    x = x_ref[...].reshape(rows, d_model)
    dy = d_ref[...].reshape(rows, d_model)
    seg = pl.ds(pl.multiple_of(half * HALF, HALF), HALF)
    rank = rank_ref[e, seg, :]
    gate = g_ref[e, seg, :]
    slot = lax.broadcasted_iota(jnp.int32, (HALF, LEVEL_ROWS, LANES), 1) + level * LEVEL_ROWS
    hit = rank[:, None, :] == slot.astype(F32)
    g_slot = jnp.sum(jnp.where(hit, gate[:, None, :], 0.0), axis=2, keepdims=True).reshape(rows, 1)

    h1 = dot_nt(x, wg_ref[...]).astype(BF16).astype(F32)
    h3 = dot_nt(x, wu_ref[...]).astype(BF16).astype(F32)
    sig = jax.nn.sigmoid(h1)
    silu = h1 * sig
    act = (silu * h3).astype(BF16)
    out = dot_nn(act, wd_ref[...])
    dyf = dy.astype(F32)
    dg = jnp.sum(out * dyf, axis=1, keepdims=True)
    go_ref[...] = (out * g_slot).astype(BF16).reshape(go_ref.shape)
    do = (dyf * g_slot).astype(BF16)
    da = dot_nt(do, wd_ref[...]).astype(BF16).astype(F32)
    dh1 = (da * h3 * sig * (1.0 + h1 * (1.0 - sig))).astype(BF16)
    dh3 = (da * silu).astype(BF16)
    dx = dot_nn(dh1, wg_ref[...]) + dot_nn(dh3, wu_ref[...])
    dx_ref[...] = dx.astype(BF16).reshape(dx_ref.shape)
    dg_tok = jnp.sum(jnp.where(hit, dg.reshape(HALF, LEVEL_ROWS, 1), 0.0), axis=1)

    @pl.when(i == 0)
    def _():
        dg_ref[...] = jnp.zeros(dg_ref.shape, F32)

    dg_ref[e, seg, :] += dg_tok

    @pl.when(fresh)
    def _():
        dwd_ref[...] = dot_tn(act, do)
        dwg_ref[...] = dot_tn(dh1, x)
        dwu_ref[...] = dot_tn(dh3, x)

    @pl.when(jnp.logical_not(fresh))
    def _():
        dwd_ref[...] += dot_tn(act, do)
        dwg_ref[...] += dot_tn(dh1, x)
        dwu_ref[...] += dot_tn(dh3, x)


def scatter_kernel(go_ref, dx_ref, uall_ref, rank_ref, dgb_ref, prob_ref, gown_ref, u_ref, dy_ref, wr_ref,
                   yo_ref, du_ref, dwr_ref,
                   slots, pbuf, acc, sib_out, sib_in, y_out, y_in, z_out, z_in, dg_in, dl_all, ubuf,
                   ld_sem, sib_ss, sib_rs, y_ss, y_rs, z_ss, z_rs, dg_ss, dg_rs, dl_ss, dl_rs, u_sem):
    y, c, z = position()
    me = block_of(y, c, z)
    ep_me = y * 2 + c
    ep_sib = y * 2 + 1 - c
    ep_y = (1 - y) * 2 + c
    blocks, local, lanes = rank_ref.shape
    tok, d_model = u_ref.shape
    cap = pbuf.shape[0] // local
    experts = prob_ref.shape[0]

    def dg_copy(s, src):
        return pltpu.make_async_remote_copy(
            src_ref=dgb_ref.at[s], dst_ref=dg_in.at[src], send_sem=dg_ss.at[s], recv_sem=dg_rs.at[src],
            device_id={"ep": s // 4, "etp": s % 4}, device_id_type=MESH)

    def dl_copy(s, src):
        return pltpu.make_async_remote_copy(
            src_ref=dl_all.at[src], dst_ref=dl_all.at[src], send_sem=dl_ss.at[s], recv_sem=dl_rs.at[src],
            device_id={"ep": s // 4, "etp": s % 4}, device_id_type=MESH)

    def sib_copy(slot, arr, k):
        return pltpu.make_async_remote_copy(
            src_ref=sib_out.at[slot], dst_ref=sib_in.at[arr, k], send_sem=sib_ss.at[slot], recv_sem=sib_rs.at[arr, k],
            device_id={"ep": ep_sib, "etp": z}, device_id_type=MESH)

    def y_copy(arr, k):
        return pltpu.make_async_remote_copy(
            src_ref=y_out.at[arr, k], dst_ref=y_in.at[arr, k], send_sem=y_ss.at[arr, k], recv_sem=y_rs.at[arr, k],
            device_id={"ep": ep_y, "etp": z}, device_id_type=MESH)

    def z_copy(arr, k, slot, z_to):
        return pltpu.make_async_remote_copy(
            src_ref=z_out.at[arr, k], dst_ref=z_in.at[arr, slot], send_sem=z_ss.at[arr, k], recv_sem=z_rs.at[arr, slot],
            device_id={"ep": ep_me, "etp": z_to}, device_id_type=MESH)

    def plan(n):
        arr = jnp.where(n < 12, 0, jnp.where(n < 20, 1, jnp.where(n < 24, 0, 1)))
        phase = jnp.where(n < 8, 1, jnp.where(n < 12, 2, jnp.where(n < 20, 1, jnp.where(n < 24, 3, jnp.where(n < 28, 2, 3)))))
        off = jnp.where(n < 8, n, n % 4)
        off = jnp.where((n >= 12) & (n < 20), n - 12, off)
        k = jnp.where(phase == 1, off // 2, off)
        to_sib = jnp.where(phase == 1, 1 - off % 2, jnp.where(phase == 2, 1, 0))
        other = jnp.where(phase == 1, 1, 0)
        core = c + to_sib - 2 * c * to_sib
        col = y + other - 2 * y * other
        return arr, phase, k, to_sib, block_of(col, core, far_order(z, k))

    def start_load(n, slot):
        arr, phase, k, to_sib, s = plan(n)

        @pl.when(arr == 0)
        def _():
            pltpu.make_async_copy(go_ref.at[s], slots.at[slot], ld_sem.at[slot]).start()

        @pl.when(arr == 1)
        def _():
            pltpu.make_async_copy(dx_ref.at[s], slots.at[slot], ld_sem.at[slot]).start()

    start_load(0, 0)

    @pl.loop(1, blocks)
    def _(i):
        dg_copy((me + i) % blocks, me).start()

    dg_in[me] = dgb_ref[me]

    @pl.loop(0, 32)
    def _(n):
        slot = n % 2
        arr, phase, k, to_sib, s = plan(n)

        @pl.when(n < 31)
        def _():
            start_load(n + 1, 1 - slot)

        pbuf[...] = one_hot_slots(rank_ref[s][:, 0:tok], cap)
        pltpu.make_async_copy(go_ref.at[s], slots.at[slot], ld_sem.at[slot]).wait()

        @pl.loop(0, d_model // CHUNK)
        def _(m):
            cols = pl.ds(pl.multiple_of(m * CHUNK, CHUNK), CHUNK)
            acc[:, cols] = dot_tn(pbuf[...], slots[slot, :, cols])

        @pl.when(to_sib == 1)
        def _():
            idx = k + 4 * (phase - 1)
            out = idx % 2

            @pl.when((idx >= 2) | (arr == 1))
            def _():
                sib_copy(out, arr, idx).wait_send()

            sib_out[out] = acc[...].astype(BF16)
            sib_copy(out, arr, idx).start()

        @pl.when((phase == 1) & (to_sib == 0))
        def _():
            sib_copy(0, arr, k).wait_recv()
            y_out[arr, k] = (acc[...] + sib_in[arr, k].astype(F32)).astype(BF16)
            y_copy(arr, k).start()

        @pl.when(phase == 3)
        def _():
            sib_copy(0, arr, k + 4).wait_recv()
            y_copy(arr, k).wait_recv()
            acc[...] = acc[...] + sib_in[arr, k + 4].astype(F32) + y_in[arr, k].astype(F32)
            target = far_order(z, k)

            @pl.when(((target > z) & (z > 0)) | ((target < z) & (z < 3)) | ((target == z) & (z > 0)))
            def _():
                z_copy(arr, 0, target, z).wait_recv()
                acc[...] += z_in[arr, target].astype(F32)

            @pl.when((target == z) & (z < 3))
            def _():
                z_copy(arr, 0, 4, z).wait_recv()
                acc[...] += z_in[arr, 4].astype(F32)

            @pl.when(k < 3)
            def _():
                z_out[arr, k] = acc[...].astype(BF16)
                z_to = jnp.where(target > z, z + 1, z - 1)
                dst = jnp.where(target == z - 1, 4, target)
                z_copy(arr, k, dst, z_to).start()

            @pl.when((k == 3) & (arr == 0))
            def _():
                yo_ref[...] = (u_ref[...].astype(F32) + acc[...]).astype(BF16)

            @pl.when((k == 3) & (arr == 1))
            def _():
                dl3 = split3(dl_all[me][:, 0:tok])
                wr = wr_ref[...]
                router = dot_tn(dl3, jnp.concatenate([wr, wr, wr], axis=0))
                du_ref[...] = (dy_ref[...].astype(F32) + acc[...] + router).astype(BF16)

        @pl.when(n == 11)
        def _():
            @pl.loop(0, blocks)
            def _(b):
                @pl.when(b != me)
                def _():
                    dg_copy(me, b).wait_recv()

            d_gate = jnp.sum(dg_in[...].reshape(4, 4, local, lanes), axis=1).reshape(experts, lanes)
            d_prob = jnp.where(gown_ref[...] >= 0.0, d_gate, 0.0)
            prob = prob_ref[...]
            dl_all[me] = prob * (d_prob - jnp.sum(prob * d_prob, axis=0, keepdims=True))

            @pl.loop(1, blocks)
            def _(b):
                dl_copy((me + b) % blocks, me).start()

        @pl.when(n == 27)
        def _():
            dwr_ref[...] = jnp.zeros(dwr_ref.shape, F32)
            pltpu.make_async_copy(uall_ref.at[0], ubuf.at[0], u_sem.at[0]).start()

            @pl.loop(0, blocks)
            def _(b):
                us = b % 2

                @pl.when(b < blocks - 1)
                def _():
                    pltpu.make_async_copy(uall_ref.at[b + 1], ubuf.at[1 - us], u_sem.at[1 - us]).start()

                @pl.when(b != me)
                def _():
                    dl_copy(me, b).wait_recv()

                pltpu.make_async_copy(uall_ref.at[b], ubuf.at[us], u_sem.at[us]).wait()
                part = dot_nn(split3(dl_all[b][:, 0:tok]), ubuf[us])
                dwr_ref[...] += part[0:experts] + part[experts:2 * experts] + part[2 * experts:3 * experts]

    for out in (0, 1):
        sib_copy(out, 0, 0).wait_send()

    @pl.loop(0, 4)
    def _(k):
        for arr in (0, 1):
            y_copy(arr, k).wait_send()

            @pl.when(k < 3)
            def _():
                z_copy(arr, k, 0, z).wait_send()

    @pl.loop(0, blocks)
    def _(b):
        @pl.when(b != me)
        def _():
            dg_copy(b, me).wait_send()
            dl_copy(b, me).wait_send()


def work_list(rank, cap):
    local, blocks, lanes = rank.shape
    levels = cap // LEVEL_ROWS
    halves = blocks // HALF
    top = jnp.max(rank.reshape(local, halves, HALF * lanes), axis=2).astype(jnp.int32)
    level = jnp.arange(levels, dtype=jnp.int32)
    active = (level[None, :, None] * LEVEL_ROWS <= top[:, None, :]) | (level[None, :, None] == 0)
    flat = active.reshape(-1).astype(jnp.int32)
    total = flat.shape[0]
    idx = jnp.arange(total, dtype=jnp.int32)
    pos = jnp.sum(jnp.where(idx[None, :] < idx[:, None], flat[None, :], 0), axis=1)
    count = jnp.sum(flat)
    want = jnp.minimum(idx, count - 1)
    hit = (pos[None, :] == want[:, None]) & (flat[None, :] == 1)
    order = jnp.sum(jnp.where(hit, idx[None, :], 0), axis=1)
    return order // (levels * halves), (order // halves) % levels, order % halves, count.reshape(1)


def solution(mesh):
    ep_size = mesh.shape["ep"]
    etp_size = mesh.shape["etp"]
    blocks = ep_size * etp_size
    tok_spec = P(("dp", "ep", "etp"), None)
    col_spec = P("ep", None, "etp")
    row_spec = P("ep", "etp", None)
    in_specs = (tok_spec, tok_spec, tok_spec, P(None, None), col_spec, col_spec, row_spec)
    out_specs = (tok_spec, tok_spec, P(("dp", "ep"), None, "etp"), P(("dp", "ep"), None, "etp"), P(("dp", "ep"), "etp", None), P("dp", None))
    any_spec = pl.BlockSpec(memory_space=pl.ANY)
    vmem = pl.BlockSpec(memory_space=pltpu.VMEM)
    dma = pltpu.SemaphoreType.DMA

    def device_step(u_loc, dy_loc, ids_loc, w_router, w_gate, w_up, w_down):
        tok, d_model = u_loc.shape
        top_k = ids_loc.shape[1]
        experts = w_router.shape[1]
        local = w_gate.shape[0]
        ffn = w_gate.shape[2]
        cap = 96
        slots = local * cap
        ids_t = ids_loc.T
        wr_t = w_router.T
        wg_t = jnp.swapaxes(w_gate, 1, 2)
        wu_t = jnp.swapaxes(w_up, 1, 2)

        slot_shape = jax.ShapeDtypeStruct((blocks, slots, d_model), BF16)
        meta_shape = jax.ShapeDtypeStruct((blocks, local, LANES), F32)
        own_shape = jax.ShapeDtypeStruct((experts, LANES), F32)
        x_slots, d_slots, u_all, rank, gate, prob, g_own = pl.pallas_call(
            gather_kernel,
            name="gather",
            out_shape=(slot_shape, slot_shape, jax.ShapeDtypeStruct((blocks, tok, d_model), BF16), meta_shape, meta_shape, own_shape, own_shape),
            in_specs=[any_spec, any_spec, vmem, vmem],
            out_specs=(any_spec, any_spec, any_spec, vmem, vmem, vmem, vmem),
            scratch_shapes=[
                pltpu.VMEM((2, blocks, tok, d_model), BF16),
                pltpu.VMEM((slots, tok), BF16),
                pltpu.VMEM((2, slots, d_model), BF16),
                dma((2,)), dma((2, blocks, 4)), dma((2, blocks)), dma((blocks,)), dma((blocks,)), dma((2,)), dma((blocks,)),
            ],
            compiler_params=pltpu.CompilerParams(has_side_effects=True, vmem_limit_bytes=60 * 1024 * 1024),
        )(u_loc, dy_loc, ids_t, wr_t)

        rank_e = jnp.swapaxes(rank, 0, 1)
        gate_e = jnp.swapaxes(gate, 0, 1)
        te, tl, th, count = work_list(rank_e, cap)
        levels = cap // LEVEL_ROWS
        tiles = (blocks, local, levels, LEVEL_ROWS, d_model)

        def tile_map(i, te, tl, th, count):
            return th[i], te[i], tl[i], 0, 0

        def weight_map(i, te, tl, th, count):
            return te[i], 0, 0

        def whole(i, te, tl, th, count):
            return 0, 0, 0

        tile_spec = pl.BlockSpec((HALF, None, None, LEVEL_ROWS, d_model), tile_map)
        weight_spec = pl.BlockSpec((None, ffn, d_model), weight_map)
        meta_spec = pl.BlockSpec((local, blocks, LANES), whole)
        dw_shape = jax.ShapeDtypeStruct((local, ffn, d_model), F32)
        tile_shape = jax.ShapeDtypeStruct(tiles, BF16)
        go, dx, dwg, dwu, dwd, dg = pl.pallas_call(
            expert_kernel,
            name="experts",
            out_shape=(tile_shape, tile_shape, dw_shape, dw_shape, dw_shape, jax.ShapeDtypeStruct((local, blocks, LANES), F32)),
            grid_spec=pltpu.PrefetchScalarGridSpec(
                num_scalar_prefetch=4,
                grid=(local * levels * (blocks // HALF),),
                in_specs=[tile_spec, tile_spec, weight_spec, weight_spec, weight_spec, meta_spec, meta_spec],
                out_specs=[tile_spec, tile_spec, weight_spec, weight_spec, weight_spec, meta_spec],
            ),
            input_output_aliases={4: 0, 5: 1},
            compiler_params=pltpu.CompilerParams(vmem_limit_bytes=60 * 1024 * 1024, dimension_semantics=("arbitrary",)),
        )(te, tl, th, count, x_slots.reshape(tiles), d_slots.reshape(tiles), wg_t, wu_t, w_down, rank_e, gate_e)

        dg_blocks = jnp.swapaxes(dg, 0, 1)
        y_loc, du_loc, dwr_t = pl.pallas_call(
            scatter_kernel,
            name="scatter",
            out_shape=(jax.ShapeDtypeStruct((tok, d_model), BF16), jax.ShapeDtypeStruct((tok, d_model), BF16), jax.ShapeDtypeStruct((experts, d_model), F32)),
            in_specs=[any_spec, any_spec, any_spec] + [vmem] * 7,
            out_specs=(vmem, vmem, vmem),
            scratch_shapes=[
                pltpu.VMEM((2, slots, d_model), BF16),
                pltpu.VMEM((slots, tok), BF16),
                pltpu.VMEM((tok, d_model), F32),
                pltpu.VMEM((2, tok, d_model), BF16),
                pltpu.VMEM((2, 8, tok, d_model), BF16),
                pltpu.VMEM((2, 4, tok, d_model), BF16),
                pltpu.VMEM((2, 4, tok, d_model), BF16),
                pltpu.VMEM((2, 3, tok, d_model), BF16),
                pltpu.VMEM((2, 5, tok, d_model), BF16),
                pltpu.VMEM((blocks, local, LANES), F32),
                pltpu.VMEM((blocks, experts, LANES), F32),
                pltpu.VMEM((2, tok, d_model), BF16),
                dma((2,)), dma((2,)), dma((2, 8)), dma((2, 4)), dma((2, 4)), dma((2, 3)), dma((2, 5)),
                dma((blocks,)), dma((blocks,)), dma((blocks,)), dma((blocks,)), dma((2,)),
            ],
            compiler_params=pltpu.CompilerParams(has_side_effects=True, vmem_limit_bytes=60 * 1024 * 1024),
        )(go.reshape(slot_shape.shape), dx.reshape(slot_shape.shape), u_all, rank, dg_blocks, prob, g_own, u_loc, dy_loc, wr_t)

        dw_gate = jnp.swapaxes(dwg, 1, 2)
        dw_up = jnp.swapaxes(dwu, 1, 2)
        return y_loc, du_loc, dw_gate, dw_up, dwd, dwr_t.T

    return jax.shard_map(device_step, mesh=mesh, in_specs=in_specs, out_specs=out_specs, check_vma=False)
```

time: 2630 us -> 387 us (0.15)
  waiting for transfers between devices: 930 us -> 0 us
  blocking collectives: 883 us -> 0 us
  local copies, waits for them, and re-layouts: 442 us -> 9.01 us
  Pallas kernels: 0 us -> 372 us
  matrix products: 243 us -> 0 us
  other arithmetic: 84.2 us -> 2.85 us
    all_to_all x2 -> x0, blocking collectives: 855 us -> none  [the longest x1 428 us: device_step(): lax.all_to_all(x_send.reshape(experts, cap_slots, d_model), 'ep', 0, 0, t...]
    all_to_all x2 -> x0, waiting for transfers between devices: 802 us -> none  [the longest x1 405 us: device_step(): lax.all_to_all(out_part.reshape(experts, cap_slots, d_model), 'ep', 0, 0,...]
    pallas_call x0 -> x3, Pallas kernels: none -> 372 us  [the longest x1 163 us: device_step(): pl.pallas_call(scatter_kernel, name='scatter', out_shape=(jax.ShapeDtypeS...]
    gather x12 -> x0, local copies, waits for them, and re-layouts: 370 us -> none  [the longest x2 81.8 us: device_step(): jnp.take(out_back.reshape(experts * cap_slots, d_model), pair_slot, axis=0)]
    dot_general x15 -> x0, matrix products: 243 us -> none  [the longest x1 40.7 us: device_step(): jnp.einsum('secf,edf->secd', d_up_h, w_up, preferred_element_type=jnp.flo...]
    psum x1 -> x0, waiting for transfers between devices: 92.6 us -> none  [device_step(): lax.psum(jnp.einsum('td,te->de', u_loc, d_logit, preferred_element_type=j...]
    convert_element_type x2 -> x1, local copies, waits for them, and re-layouts: 51.9 us -> 0.1 us  [work_list(): flat = active.reshape(-1).astype(jnp.int32)]
    convert_element_type x3 -> x2, other arithmetic: 28 us -> 0.08 us  [the longest x1 0.07 us: work_list(): flat = active.reshape(-1).astype(jnp.int32)]
  transfers between devices with their start and end apart: 8 -> 0, of which waited for: 5 -> 0; matrix products, arithmetic and copies ran while one was open for 13% -> 0% of each run, Pallas kernels for 0% -> 0%
where the time goes in v1:
time: 387 us; the launch traced here: 386 us
  Pallas kernels  372 us (96%)
  local copies, waits for them, and re-layouts  9.01 us (2%)
    pallas_call x1, Pallas kernels, device_step(): pl.pallas_call(scatter_kernel, name='scatter', out_shape=(jax.ShapeDtypeS...  163 us
    pallas_call x1, Pallas kernels, device_step(): pl.pallas_call(gather_kernel, name='gather', out_shape=(slot_shape, slot_...  124 us
    pallas_call x1, Pallas kernels, device_step(): pl.pallas_call(expert_kernel, name='experts', out_shape=(tile_shape, tile...  85.1 us

profile of v1, /device:TPU:0, one launch (start us, length us, event | category | flops | bytes accessed | tf_op | source)
XLA Modules:
  0.0 385.6 jit_solution(8423866603271577029)
XLA Ops:
  0.7 123.9 %gather.1 = (bf16[16,768,1536]{2,1,0:T(8,128)(2,1)}, bf16[16,768,1536]{2,1,0:T(8,128)(2,1)}, bf16[16,192,1536]{2,1,0:T(8,128)(2,1)}, f32[16,8,256]{2,1,0:T(8,128...) custom-call(bf16[192,1536]{1,0:T(8,128)(2,1)} %u_ref.3, bf16[192,1536]{1,0:T(8,128)(2,1)} %dy_ref.3, ...), custom_call_target="tpu_custom_call" | custom-call | tf_op jit(solution)/shard_map/gather/pallas_call | solution.py:573
  124.5 1.0 fusion.1
  125.6 0.1 reduce_max.14
  125.6 0.1 reduce_max.18
  125.7 0.8 fusion
  127.1 0.1 or_convert_fusion
  127.2 0.1 reshape.86
  127.3 0.1 select_reduce_fusion.1
  127.4 0.2 select_reduce_fusion
  127.6 0.6 and_select_fusion
  128.2 1.7 copy_bitcast_fusion.1
  130.0 85.1 %experts.1 = (bf16[16,8,3,32,1536]{4,3,2,1,0:T(8,128)(2,1)}, bf16[16,8,3,32,1536]{4,3,2,1,0:T(8,128)(2,1)}, f32[8,192,1536]{2,1,0:T(8,128)}, f32[8,192,1536]{2,1...) custom-call(s32[48]{0:T(128)} %get-tuple-element.39.te, ...), custom_call_target="tpu_custom_call", output_to_operand_aliasing={{0}: (4, {}), {1}: (5, {})} | custom-call | tf_op jit(solution)/shard_map/experts/pallas_call | solution.py:608
  215.1 1.6 copy.29
  216.7 163.4 %scatter.1 = (bf16[192,1536]{1,0:T(8,128)(2,1)}, bf16[192,1536]{1,0:T(8,128)(2,1)}, f32[32,1536]{1,0:T(8,128)}) custom-call(bf16[16,768,1536]{2,1,0:T(8,128)(2,1)} %bitcast.22, bf16[16,768,1536]{2,1,0:T(8,128)(2,1)} %bitcast.24, bf16[16,192,1536]{2,1,0:T(8,128)(2,1)} %get-tuple-element.28.uall_ref, f32[16,8,256]{2,1,0:T(8,128)} %get-tuple-element.22.rank_ref, ...), custom_call_target="tpu_custom_call" | custom-call | tf_op jit(solution)/shard_map/scatter/pallas_call | solution.py:623
  380.1 1.9 copy.35
  382.0 1.9 copy.36
  384.0 1.6 copy.37
  (5 shorter events, 0.0 us)

commit v2 on v1

--- a/solution.py
+++ b/solution.py
@@ -58,6 +58,18 @@
     return jnp.where(hit, 1.0, 0.0).reshape(experts * cap, tok).astype(BF16)
 
 
+def one_hot_tokens(rank, cap):
+    experts, tok = rank.shape
+    lane = lax.broadcasted_iota(jnp.int32, (experts, experts * cap), 1)
+    first = lax.broadcasted_iota(jnp.int32, (experts, experts * cap), 0) * cap
+    mine = (lane >= first) & (lane < first + cap)
+    spread = dot_tn(rank.astype(BF16), jnp.where(mine, 1.0, 0.0).astype(BF16))
+    row = lax.broadcasted_iota(jnp.int32, (1, experts * cap), 1)
+    for e in range(1, experts):
+        row = row - jnp.where(lane[0:1] >= e * cap, cap, 0)
+    return jnp.where(spread == row.astype(F32), 1.0, 0.0).astype(BF16)
+
+
 def split3(x):
     hi = x.astype(BF16)
     rest = x - hi.astype(F32)
@@ -66,7 +78,7 @@
     return jnp.concatenate([hi, mid, low], axis=0)
 
 
-def gather_kernel(u_ref, dy_ref, ids_ref, wr_ref, x_ref, d_ref, uall_ref, rank_ref, g_ref, prob_ref, gown_ref,
+def gather_kernel(u_ref, dy_ref, ids_ref, wr_ref, x_ref, d_ref, uall_ref, rank_ref, g_ref, prob_ref, gown_ref, cnt_ref,
                   rcv, pbuf, xbuf, in_sem, send_sem, recv_sem, meta_send, meta_recv, out_sem, uout_sem):
     y, c, z = position()
     me = block_of(y, c, z)
@@ -210,7 +222,9 @@
                     meta_wait(s).wait_recv()
 
                 mask = g_ref[s] >= 0.0
-                rank = dot_nn(jnp.where(mask, 1.0, 0.0).astype(BF16), before)
+                ones = jnp.where(mask, 1.0, 0.0)
+                rank = dot_nn(ones.astype(BF16), before)
+                cnt_ref[s] = jnp.broadcast_to(jnp.sum(ones, axis=1, keepdims=True), cnt_ref.shape[1:]).astype(jnp.int32)
                 rank_ref[s] = jnp.where(mask, rank, -1.0)
 
             pbuf[...] = one_hot_slots(rank_ref[s][:, 0:tok], cap)
@@ -222,7 +236,7 @@
             @pl.loop(0, d_model // CHUNK)
             def _(n):
                 cols = pl.ds(pl.multiple_of(n * CHUNK, CHUNK), CHUNK)
-                xbuf[slot, :, cols] = dot_nn(pbuf[...], rcv[arr, s, :, cols]).astype(BF16)
+                xbuf[slot, :, :, :, cols] = dot_nn(pbuf[...], rcv[arr, s, :, cols]).astype(BF16).reshape(xbuf.shape[1:4] + (CHUNK,))
 
             @pl.when(arr == 0)
             def _():
@@ -262,67 +276,205 @@
             send_sib(arr, sy).wait_send()
 
 
-def expert_kernel(te, tl, th, count, x_ref, d_ref, wg_ref, wu_ref, wd_ref, rank_ref, g_ref,
-                  go_ref, dx_ref, dwg_ref, dwu_ref, dwd_ref, dg_ref):
-    i = pl.program_id(0)
-
-    @pl.when(i < count[0])
-    def _():
-        expert_tile(i, te, tl, th, x_ref, d_ref, wg_ref, wu_ref, wd_ref, rank_ref, g_ref, go_ref, dx_ref, dwg_ref, dwu_ref, dwd_ref, dg_ref)
-
-
-def expert_tile(i, te, tl, th, x_ref, d_ref, wg_ref, wu_ref, wd_ref, rank_ref, g_ref,
-                go_ref, dx_ref, dwg_ref, dwu_ref, dwd_ref, dg_ref):
-    e = te[i]
-    level = tl[i]
-    half = th[i]
-    rows = HALF * LEVEL_ROWS
-    d_model = x_ref.shape[-1]
-    fresh = (i == 0) | (te[jnp.maximum(i - 1, 0)] != e)
-
-    x = x_ref[...].reshape(rows, d_model)
-    dy = d_ref[...].reshape(rows, d_model)
-    seg = pl.ds(pl.multiple_of(half * HALF, HALF), HALF)
-    rank = rank_ref[e, seg, :]
-    gate = g_ref[e, seg, :]
-    slot = lax.broadcasted_iota(jnp.int32, (HALF, LEVEL_ROWS, LANES), 1) + level * LEVEL_ROWS
-    hit = rank[:, None, :] == slot.astype(F32)
-    g_slot = jnp.sum(jnp.where(hit, gate[:, None, :], 0.0), axis=2, keepdims=True).reshape(rows, 1)
-
-    h1 = dot_nt(x, wg_ref[...]).astype(BF16).astype(F32)
-    h3 = dot_nt(x, wu_ref[...]).astype(BF16).astype(F32)
-    sig = jax.nn.sigmoid(h1)
-    silu = h1 * sig
-    act = (silu * h3).astype(BF16)
-    out = dot_nn(act, wd_ref[...])
-    dyf = dy.astype(F32)
-    dg = jnp.sum(out * dyf, axis=1, keepdims=True)
-    go_ref[...] = (out * g_slot).astype(BF16).reshape(go_ref.shape)
-    do = (dyf * g_slot).astype(BF16)
-    da = dot_nt(do, wd_ref[...]).astype(BF16).astype(F32)
-    dh1 = (da * h3 * sig * (1.0 + h1 * (1.0 - sig))).astype(BF16)
-    dh3 = (da * silu).astype(BF16)
-    dx = dot_nn(dh1, wg_ref[...]) + dot_nn(dh3, wu_ref[...])
-    dx_ref[...] = dx.astype(BF16).reshape(dx_ref.shape)
-    dg_tok = jnp.sum(jnp.where(hit, dg.reshape(HALF, LEVEL_ROWS, 1), 0.0), axis=1)
-
-    @pl.when(i == 0)
-    def _():
-        dg_ref[...] = jnp.zeros(dg_ref.shape, F32)
-
-    dg_ref[e, seg, :] += dg_tok
-
-    @pl.when(fresh)
-    def _():
-        dwd_ref[...] = dot_tn(act, do)
-        dwg_ref[...] = dot_tn(dh1, x)
-        dwu_ref[...] = dot_tn(dh3, x)
-
-    @pl.when(jnp.logical_not(fresh))
-    def _():
-        dwd_ref[...] += dot_tn(act, do)
-        dwg_ref[...] += dot_tn(dh1, x)
-        dwu_ref[...] += dot_tn(dh3, x)
+class ExpertTiles:
+    def __init__(self, x_in, d_in, go, dx, wg, wu, wd, te, tk, tn, sg, xb, db, gob, dxb, wb, in_sem, out_sem, w_sem):
+        self.te, self.tk, self.tn, self.sg = te, tk, tn, sg
+        self.x_in, self.d_in, self.go, self.dx = x_in, d_in, go, dx
+        self.w = (wg, wu, wd)
+        self.xb, self.db, self.gob, self.dxb, self.wb = xb, db, gob, dxb, wb
+        self.in_sem, self.out_sem, self.w_sem = in_sem, out_sem, w_sem
+
+    def seg(self, ref, i, j):
+        at = self.sg[i * HALF + j]
+        return ref.at[at // 4, self.te[i], at % 4]
+
+    def half(self, ref, i):
+        return ref.at[pl.ds(pl.multiple_of(self.tk[i] * HALF, HALF), HALF), self.te[i], 0]
+
+    def each(self, i, slot, act, moves, sem):
+        @pl.when(self.tk[i] < 2)
+        def _():
+            for a, (hbm, buf, out) in enumerate(moves):
+                ends = (buf.at[slot], self.half(hbm, i)) if out else (self.half(hbm, i), buf.at[slot])
+                act(pltpu.make_async_copy(*ends, sem.at[a, slot, HALF]))
+
+        for j in range(HALF):
+            @pl.when((self.tk[i] == 2) & (j < self.tn[i]))
+            def _():
+                for a, (hbm, buf, out) in enumerate(moves):
+                    ends = (buf.at[slot, j], self.seg(hbm, i, j)) if out else (self.seg(hbm, i, j), buf.at[slot, j])
+                    act(pltpu.make_async_copy(*ends, sem.at[a, slot, j]))
+
+    def load(self, i, slot, act):
+        self.each(i, slot, act, ((self.x_in, self.xb, False), (self.d_in, self.db, False)), self.in_sem)
+
+    def store(self, i, slot, act):
+        self.each(i, slot, act, ((self.go, self.gob, True), (self.dx, self.dxb, True)), self.out_sem)
+
+    def weights(self, e, p):
+        return [pltpu.make_async_copy(src.at[e], self.wb.at[p, j], self.w_sem.at[p, j]) for j, src in enumerate(self.w)]
+
+    def run(self, i, slot, p, fresh, dwb, dob, sgb, rank_ref, g_ref, dg_ref):
+        rows = HALF * LEVEL_ROWS
+        d_model = self.xb.shape[-1]
+        one = pl.ds(self.te[i], 1)
+        for j in range(HALF):
+            at = self.sg[i * HALF + j]
+            level = jnp.where(j < self.tn[i], at % 4, 8) * LEVEL_ROWS
+            sgb[0, pl.ds(j, 1), :] = rank_ref[at // 4, one, :] - level.astype(F32)
+            sgb[1, pl.ds(j, 1), :] = g_ref[at // 4, one, :]
+        row = lax.broadcasted_iota(jnp.int32, (HALF, LEVEL_ROWS, LANES), 1)
+        hit = sgb[0][:, None, :] == row.astype(F32)
+        g_slot = jnp.sum(jnp.where(hit, sgb[1][:, None, :], 0.0), axis=2, keepdims=True).reshape(rows, 1)
+        x = self.xb[slot].reshape(rows, d_model)
+        h1 = dot_nt(x, self.wb[p, 0]).astype(BF16).astype(F32)
+        h3 = dot_nt(x, self.wb[p, 1]).astype(BF16).astype(F32)
+        sig = jax.nn.sigmoid(h1)
+        silu = h1 * sig
+        act = (silu * h3).astype(BF16)
+        chunks = [slice(n, n + CHUNK) for n in range(0, d_model, CHUNK)]
+        dg = jnp.zeros((rows, 1), F32)
+        da = jnp.zeros((rows, act.shape[1]), F32)
+        for cols in chunks:
+            out = dot_nn(act, self.wb[p, 2, :, cols])
+            dy = self.db[slot, :, :, cols].reshape(rows, CHUNK).astype(F32)
+            dg = dg + jnp.sum(out * dy, axis=1, keepdims=True)
+            self.gob[slot, :, :, cols] = (out * g_slot).astype(BF16).reshape(HALF, LEVEL_ROWS, CHUNK)
+            do = (dy * g_slot).astype(BF16)
+            dob[:, cols] = do
+            da = da + dot_nt(do, self.wb[p, 2, :, cols])
+        da = da.astype(BF16).astype(F32)
+        dh1 = (da * h3 * sig * (1.0 + h1 * (1.0 - sig))).astype(BF16)
+        dh3 = (da * silu).astype(BF16)
+        for cols in chunks:
+            dx = dot_nn(dh1, self.wb[p, 0, :, cols]) + dot_nn(dh3, self.wb[p, 1, :, cols])
+            self.dxb[slot, :, :, cols] = dx.astype(BF16).reshape(HALF, LEVEL_ROWS, CHUNK)
+        sgb[0] = jnp.sum(jnp.where(hit, dg.reshape(HALF, LEVEL_ROWS, 1), 0.0), axis=1)
+        for j in range(HALF):
+            dg_ref[self.sg[i * HALF + j] // 4, one, :] += sgb[0, pl.ds(j, 1), :]
+
+        def add_dw(first):
+            for cols in chunks:
+                xc = self.xb[slot, :, :, cols].reshape(rows, CHUNK)
+                for j, (left, right) in enumerate(((dh1, xc), (dh3, xc), (act, dob[:, cols]))):
+                    part = dot_tn(left, right)
+                    dwb[p, j, :, cols] = part if first else dwb[p, j, :, cols] + part
+
+        @pl.when(fresh)
+        def _():
+            add_dw(True)
+
+        @pl.when(jnp.logical_not(fresh))
+        def _():
+            add_dw(False)
+
+
+def expert_kernel(cnt, x_hbm, d_hbm, wg_hbm, wu_hbm, wd_hbm, rank_ref, g_ref, go_hbm, dx_hbm, dwg_hbm, dwu_hbm, dwd_hbm, dg_ref,
+                  te, tk, tn, sg, xb, db, gob, dxb, wb, dwb, dob, sgb, in_sem, out_sem, w_sem, dw_sem):
+    local = wg_hbm.shape[0]
+    levels = x_hbm.shape[2]
+    blocks = x_hbm.shape[0]
+    halves = blocks // HALF
+    tiles = ExpertTiles(x_hbm, d_hbm, go_hbm, dx_hbm, wg_hbm, wu_hbm, wd_hbm, te, tk, tn, sg, xb, db, gob, dxb, wb, in_sem, out_sem, w_sem)
+
+    def start(copy):
+        copy.start()
+
+    def wait(copy):
+        copy.wait()
+
+    def dw_out(e, p):
+        return [pltpu.make_async_copy(dwb.at[p, j], dst.at[e], dw_sem.at[p, j]) for j, dst in enumerate((dwg_hbm, dwu_hbm, dwd_hbm))]
+
+    te[0] = 0
+    tk[0] = 0
+    tn[0] = HALF
+    for copy in tiles.weights(0, 0):
+        copy.start()
+    tiles.load(0, 0, start)
+    dg_ref[...] = jnp.zeros(dg_ref.shape, F32)
+
+    def add_expert(e, n):
+        for h in range(halves):
+            te[n + h] = e
+            tk[n + h] = h
+            tn[n + h] = HALF
+            for j in range(HALF):
+                sg[(n + h) * HALF + j] = (h * HALF + j) * 4
+        n = n + halves
+
+        def add_block(b, m):
+            held = cnt[b, e]
+            for level in range(1, levels):
+                sg[n * HALF + m] = b * 4 + level
+                m = m + jnp.where(held > level * LEVEL_ROWS, 1, 0)
+            return m
+
+        m = lax.fori_loop(0, blocks, add_block, 0)
+        for j in range(HALF):
+            sg[n * HALF + m + j] = 0
+        extra = (m + HALF - 1) // HALF
+
+        def add_tile(k, carry):
+            te[n + k] = e
+            tk[n + k] = 2
+            tn[n + k] = jnp.minimum(m - k * HALF, HALF)
+            return carry
+
+        lax.fori_loop(0, extra, add_tile, 0)
+        return n + extra
+
+    count = lax.fori_loop(0, local, add_expert, 0)
+    te[count] = local
+
+    def step(i, carry):
+        slot = i % 2
+        e = te[i]
+        p = e % 2
+        fresh = (i == 0) | (te[jnp.maximum(i - 1, 0)] != e)
+        last = te[i + 1] != e
+
+        @pl.when(i + 1 < count)
+        def _():
+            tiles.load(i + 1, 1 - slot, start)
+
+        @pl.when(fresh)
+        def _():
+            @pl.when(e + 1 < local)
+            def _():
+                for copy in tiles.weights(e + 1, 1 - p):
+                    copy.start()
+
+            for copy in tiles.weights(e, p):
+                copy.wait()
+
+            @pl.when(e >= 2)
+            def _():
+                for copy in dw_out(e, p):
+                    copy.wait()
+
+        tiles.load(i, slot, wait)
+
+        @pl.when(i >= 2)
+        def _():
+            tiles.store(i - 2, slot, wait)
+
+        tiles.run(i, slot, p, fresh, dwb, dob, sgb, rank_ref, g_ref, dg_ref)
+        tiles.store(i, slot, start)
+
+        @pl.when(last)
+        def _():
+            for copy in dw_out(e, p):
+                copy.start()
+
+        return carry
+
+    lax.fori_loop(0, count, step, 0)
+    for p in (0, 1):
+        i = count - 2 + p
+        tiles.store(i, i % 2, wait)
+        for copy in dw_out(0, p):
+            copy.wait()
 
 
 def scatter_kernel(go_ref, dx_ref, uall_ref, rank_ref, dgb_ref, prob_ref, gown_ref, u_ref, dy_ref, wr_ref,
@@ -336,7 +488,7 @@
     ep_y = (1 - y) * 2 + c
     blocks, local, lanes = rank_ref.shape
     tok, d_model = u_ref.shape
-    cap = pbuf.shape[0] // local
+    cap = pbuf.shape[1] // local
     experts = prob_ref.shape[0]
 
     def dg_copy(s, src):
@@ -394,6 +546,10 @@
         dg_copy((me + i) % blocks, me).start()
 
     dg_in[me] = dgb_ref[me]
+    dwr_ref[...] = jnp.zeros(dwr_ref.shape, F32)
+
+    def u_load(b):
+        return pltpu.make_async_copy(uall_ref.at[b], ubuf.at[b % 2], u_sem.at[b % 2])
 
     @pl.loop(0, 32)
     def _(n):
@@ -404,68 +560,15 @@
         def _():
             start_load(n + 1, 1 - slot)
 
-        pbuf[...] = one_hot_slots(rank_ref[s][:, 0:tok], cap)
+        pbuf[...] = one_hot_tokens(rank_ref[s][:, 0:tok], cap)
         pltpu.make_async_copy(go_ref.at[s], slots.at[slot], ld_sem.at[slot]).wait()
 
         @pl.loop(0, d_model // CHUNK)
         def _(m):
             cols = pl.ds(pl.multiple_of(m * CHUNK, CHUNK), CHUNK)
-            acc[:, cols] = dot_tn(pbuf[...], slots[slot, :, cols])
-
-        @pl.when(to_sib == 1)
-        def _():
-            idx = k + 4 * (phase - 1)
-            out = idx % 2
-
-            @pl.when((idx >= 2) | (arr == 1))
-            def _():
-                sib_copy(out, arr, idx).wait_send()
-
-            sib_out[out] = acc[...].astype(BF16)
-            sib_copy(out, arr, idx).start()
-
-        @pl.when((phase == 1) & (to_sib == 0))
-        def _():
-            sib_copy(0, arr, k).wait_recv()
-            y_out[arr, k] = (acc[...] + sib_in[arr, k].astype(F32)).astype(BF16)
-            y_copy(arr, k).start()
-
-        @pl.when(phase == 3)
-        def _():
-            sib_copy(0, arr, k + 4).wait_recv()
-            y_copy(arr, k).wait_recv()
-            acc[...] = acc[...] + sib_in[arr, k + 4].astype(F32) + y_in[arr, k].astype(F32)
-            target = far_order(z, k)
-
-            @pl.when(((target > z) & (z > 0)) | ((target < z) & (z < 3)) | ((target == z) & (z > 0)))
-            def _():
-                z_copy(arr, 0, target, z).wait_recv()
-                acc[...] += z_in[arr, target].astype(F32)
-
-            @pl.when((target == z) & (z < 3))
-            def _():
-                z_copy(arr, 0, 4, z).wait_recv()
-                acc[...] += z_in[arr, 4].astype(F32)
-
-            @pl.when(k < 3)
-            def _():
-                z_out[arr, k] = acc[...].astype(BF16)
-                z_to = jnp.where(target > z, z + 1, z - 1)
-                dst = jnp.where(target == z - 1, 4, target)
-                z_copy(arr, k, dst, z_to).start()
-
-            @pl.when((k == 3) & (arr == 0))
-            def _():
-                yo_ref[...] = (u_ref[...].astype(F32) + acc[...]).astype(BF16)
-
-            @pl.when((k == 3) & (arr == 1))
-            def _():
-                dl3 = split3(dl_all[me][:, 0:tok])
-                wr = wr_ref[...]
-                router = dot_tn(dl3, jnp.concatenate([wr, wr, wr], axis=0))
-                du_ref[...] = (dy_ref[...].astype(F32) + acc[...] + router).astype(BF16)
-
-        @pl.when(n == 11)
+            acc[:, cols] = dot_nn(pbuf[...], slots[slot, :, cols])
+
+        @pl.when(n == 1)
         def _():
             @pl.loop(0, blocks)
             def _(b):
@@ -482,26 +585,74 @@
             def _(b):
                 dl_copy((me + b) % blocks, me).start()
 
-        @pl.when(n == 27)
-        def _():
-            dwr_ref[...] = jnp.zeros(dwr_ref.shape, F32)
-            pltpu.make_async_copy(uall_ref.at[0], ubuf.at[0], u_sem.at[0]).start()
-
-            @pl.loop(0, blocks)
-            def _(b):
-                us = b % 2
-
-                @pl.when(b < blocks - 1)
-                def _():
-                    pltpu.make_async_copy(uall_ref.at[b + 1], ubuf.at[1 - us], u_sem.at[1 - us]).start()
-
-                @pl.when(b != me)
-                def _():
-                    dl_copy(me, b).wait_recv()
-
-                pltpu.make_async_copy(uall_ref.at[b], ubuf.at[us], u_sem.at[us]).wait()
-                part = dot_nn(split3(dl_all[b][:, 0:tok]), ubuf[us])
-                dwr_ref[...] += part[0:experts] + part[experts:2 * experts] + part[2 * experts:3 * experts]
+        @pl.when(to_sib == 1)
+        def _():
+            idx = k + 4 * (phase - 1)
+            out = idx % 2
+
+            @pl.when((idx >= 2) | (arr == 1))
+            def _():
+                sib_copy(out, arr, idx).wait_send()
+
+            sib_out[out] = acc[...].astype(BF16)
+            sib_copy(out, arr, idx).start()
+
+        @pl.when((phase == 1) & (to_sib == 0))
+        def _():
+            sib_copy(0, arr, k).wait_recv()
+            y_out[arr, k] = (acc[...] + sib_in[arr, k].astype(F32)).astype(BF16)
+            y_copy(arr, k).start()
+
+        @pl.when(phase == 3)
+        def _():
+            sib_copy(0, arr, k + 4).wait_recv()
+            y_copy(arr, k).wait_recv()
+            acc[...] = acc[...] + sib_in[arr, k + 4].astype(F32) + y_in[arr, k].astype(F32)
+            target = far_order(z, k)
+
+            @pl.when(((target > z) & (z > 0)) | ((target < z) & (z < 3)) | ((target == z) & (z > 0)))
+            def _():
+                z_copy(arr, 0, target, z).wait_recv()
+                acc[...] += z_in[arr, target].astype(F32)
+
+            @pl.when((target == z) & (z < 3))
+            def _():
+                z_copy(arr, 0, 4, z).wait_recv()
+                acc[...] += z_in[arr, 4].astype(F32)
+
+            @pl.when(k < 3)
+            def _():
+                z_out[arr, k] = acc[...].astype(BF16)
+                z_to = jnp.where(target > z, z + 1, z - 1)
+                dst = jnp.where(target == z - 1, 4, target)
+                z_copy(arr, k, dst, z_to).start()
+
+            @pl.when((k == 3) & (arr == 0))
+            def _():
+                yo_ref[...] = (u_ref[...].astype(F32) + acc[...]).astype(BF16)
+
+            @pl.when((k == 3) & (arr == 1))
+            def _():
+                dl3 = split3(dl_all[me][:, 0:tok])
+                wr = wr_ref[...]
+                router = dot_tn(dl3, jnp.concatenate([wr, wr, wr], axis=0))
+                du_ref[...] = (dy_ref[...].astype(F32) + acc[...] + router).astype(BF16)
+
+        @pl.when((n >= 11) & (n < 27))
+        def _():
+            u_load(n - 11).start()
+
+        @pl.when((n >= 12) & (n < 28))
+        def _():
+            b = n - 12
+
+            @pl.when(b != me)
+            def _():
+                dl_copy(me, b).wait_recv()
+
+            u_load(b).wait()
+            part = dot_nn(split3(dl_all[b][:, 0:tok]), ubuf[b % 2])
+            dwr_ref[...] += part[0:experts] + part[experts:2 * experts] + part[2 * experts:3 * experts]
 
     for out in (0, 1):
         sib_copy(out, 0, 0).wait_send()
@@ -521,24 +672,6 @@
         def _():
             dg_copy(b, me).wait_send()
             dl_copy(b, me).wait_send()
-
-
-def work_list(rank, cap):
-    local, blocks, lanes = rank.shape
-    levels = cap // LEVEL_ROWS
-    halves = blocks // HALF
-    top = jnp.max(rank.reshape(local, halves, HALF * lanes), axis=2).astype(jnp.int32)
-    level = jnp.arange(levels, dtype=jnp.int32)
-    active = (level[None, :, None] * LEVEL_ROWS <= top[:, None, :]) | (level[None, :, None] == 0)
-    flat = active.reshape(-1).astype(jnp.int32)
-    total = flat.shape[0]
-    idx = jnp.arange(total, dtype=jnp.int32)
-    pos = jnp.sum(jnp.where(idx[None, :] < idx[:, None], flat[None, :], 0), axis=1)
-    count = jnp.sum(flat)
-    want = jnp.minimum(idx, count - 1)
-    hit = (pos[None, :] == want[:, None]) & (flat[None, :] == 1)
-    order = jnp.sum(jnp.where(hit, idx[None, :], 0), axis=1)
-    return order // (levels * halves), (order // halves) % levels, order % halves, count.reshape(1)
 
 
 def solution(mesh):
@@ -567,59 +700,50 @@
         wg_t = jnp.swapaxes(w_gate, 1, 2)
         wu_t = jnp.swapaxes(w_up, 1, 2)
 
-        slot_shape = jax.ShapeDtypeStruct((blocks, slots, d_model), BF16)
+        levels = cap // LEVEL_ROWS
+        tile_shape = jax.ShapeDtypeStruct((blocks, local, levels, LEVEL_ROWS, d_model), BF16)
+        dw_shape = jax.ShapeDtypeStruct((local, ffn, d_model), F32)
         meta_shape = jax.ShapeDtypeStruct((blocks, local, LANES), F32)
         own_shape = jax.ShapeDtypeStruct((experts, LANES), F32)
-        x_slots, d_slots, u_all, rank, gate, prob, g_own = pl.pallas_call(
+        tile_buf = pltpu.VMEM((2, HALF, LEVEL_ROWS, d_model), BF16)
+        weight_buf = pltpu.VMEM((2, 3, ffn, d_model), BF16)
+        x_slots, d_slots, u_all, rank, gate, prob, g_own, counts = pl.pallas_call(
             gather_kernel,
             name="gather",
-            out_shape=(slot_shape, slot_shape, jax.ShapeDtypeStruct((blocks, tok, d_model), BF16), meta_shape, meta_shape, own_shape, own_shape),
+            out_shape=(tile_shape, tile_shape, jax.ShapeDtypeStruct((blocks, tok, d_model), BF16), meta_shape, meta_shape, own_shape, own_shape,
+                       jax.ShapeDtypeStruct((blocks, local, 128), jnp.int32)),
             in_specs=[any_spec, any_spec, vmem, vmem],
-            out_specs=(any_spec, any_spec, any_spec, vmem, vmem, vmem, vmem),
+            out_specs=(any_spec, any_spec, any_spec, vmem, vmem, vmem, vmem, vmem),
             scratch_shapes=[
                 pltpu.VMEM((2, blocks, tok, d_model), BF16),
                 pltpu.VMEM((slots, tok), BF16),
-                pltpu.VMEM((2, slots, d_model), BF16),
+                pltpu.VMEM((2, local, levels, LEVEL_ROWS, d_model), BF16),
                 dma((2,)), dma((2, blocks, 4)), dma((2, blocks)), dma((blocks,)), dma((blocks,)), dma((2,)), dma((blocks,)),
             ],
             compiler_params=pltpu.CompilerParams(has_side_effects=True, vmem_limit_bytes=60 * 1024 * 1024),
         )(u_loc, dy_loc, ids_t, wr_t)
 
-        rank_e = jnp.swapaxes(rank, 0, 1)
-        gate_e = jnp.swapaxes(gate, 0, 1)
-        te, tl, th, count = work_list(rank_e, cap)
-        levels = cap // LEVEL_ROWS
-        tiles = (blocks, local, levels, LEVEL_ROWS, d_model)
-
-        def tile_map(i, te, tl, th, count):
-            return th[i], te[i], tl[i], 0, 0
-
-        def weight_map(i, te, tl, th, count):
-            return te[i], 0, 0
-
-        def whole(i, te, tl, th, count):
-            return 0, 0, 0
-
-        tile_spec = pl.BlockSpec((HALF, None, None, LEVEL_ROWS, d_model), tile_map)
-        weight_spec = pl.BlockSpec((None, ffn, d_model), weight_map)
-        meta_spec = pl.BlockSpec((local, blocks, LANES), whole)
-        dw_shape = jax.ShapeDtypeStruct((local, ffn, d_model), F32)
-        tile_shape = jax.ShapeDtypeStruct(tiles, BF16)
-        go, dx, dwg, dwu, dwd, dg = pl.pallas_call(
+        max_tiles = local * levels * (blocks // HALF) + 8
+        smem_list = pltpu.SMEM((max_tiles,), jnp.int32)
+        smem = pl.BlockSpec(memory_space=pltpu.SMEM)
+        go, dx, dwg, dwu, dwd, dg_blocks = pl.pallas_call(
             expert_kernel,
             name="experts",
-            out_shape=(tile_shape, tile_shape, dw_shape, dw_shape, dw_shape, jax.ShapeDtypeStruct((local, blocks, LANES), F32)),
-            grid_spec=pltpu.PrefetchScalarGridSpec(
-                num_scalar_prefetch=4,
-                grid=(local * levels * (blocks // HALF),),
-                in_specs=[tile_spec, tile_spec, weight_spec, weight_spec, weight_spec, meta_spec, meta_spec],
-                out_specs=[tile_spec, tile_spec, weight_spec, weight_spec, weight_spec, meta_spec],
-            ),
-            input_output_aliases={4: 0, 5: 1},
-            compiler_params=pltpu.CompilerParams(vmem_limit_bytes=60 * 1024 * 1024, dimension_semantics=("arbitrary",)),
-        )(te, tl, th, count, x_slots.reshape(tiles), d_slots.reshape(tiles), wg_t, wu_t, w_down, rank_e, gate_e)
-
-        dg_blocks = jnp.swapaxes(dg, 0, 1)
+            out_shape=(tile_shape, tile_shape, dw_shape, dw_shape, dw_shape, meta_shape),
+            in_specs=[smem] + [any_spec] * 5 + [vmem] * 2,
+            out_specs=(any_spec,) * 5 + (vmem,),
+            scratch_shapes=[
+                smem_list, smem_list, smem_list, pltpu.SMEM((max_tiles * HALF,), jnp.int32), tile_buf, tile_buf, tile_buf, tile_buf, weight_buf,
+                pltpu.VMEM((2, 3, ffn, d_model), F32),
+                pltpu.VMEM((HALF * LEVEL_ROWS, d_model), BF16),
+                pltpu.VMEM((2, HALF, LANES), F32),
+                dma((2, 2, HALF + 1)), dma((2, 2, HALF + 1)), dma((2, 3)), dma((2, 3)),
+            ],
+            input_output_aliases={1: 0, 2: 1},
+            compiler_params=pltpu.CompilerParams(vmem_limit_bytes=60 * 1024 * 1024),
+        )(counts[:, :, 0], x_slots, d_slots, wg_t, wu_t, w_down, rank, gate)
+
+        slot_shape = (blocks, slots, d_model)
         y_loc, du_loc, dwr_t = pl.pallas_call(
             scatter_kernel,
             name="scatter",
@@ -628,7 +752,7 @@
             out_specs=(vmem, vmem, vmem),
             scratch_shapes=[
                 pltpu.VMEM((2, slots, d_model), BF16),
-                pltpu.VMEM((slots, tok), BF16),
+                pltpu.VMEM((tok, slots), BF16),
                 pltpu.VMEM((tok, d_model), F32),
                 pltpu.VMEM((2, tok, d_model), BF16),
                 pltpu.VMEM((2, 8, tok, d_model), BF16),
@@ -643,7 +767,7 @@
                 dma((blocks,)), dma((blocks,)), dma((blocks,)), dma((blocks,)), dma((2,)),
             ],
             compiler_params=pltpu.CompilerParams(has_side_effects=True, vmem_limit_bytes=60 * 1024 * 1024),
-        )(go.reshape(slot_shape.shape), dx.reshape(slot_shape.shape), u_all, rank, dg_blocks, prob, g_own, u_loc, dy_loc, wr_t)
+        )(go.reshape(slot_shape), dx.reshape(slot_shape), u_all, rank, dg_blocks, prob, g_own, u_loc, dy_loc, wr_t)
 
         dw_gate = jnp.swapaxes(dwg, 1, 2)
         dw_up = jnp.swapaxes(dwu, 1, 2)

time: 387 us -> 338 us (0.87)
  Pallas kernels: 372 us -> 331 us
    pallas_call x1, Pallas kernels: 163 us -> 140 us  [device_step(): pl.pallas_call(scatter_kernel, name='scatter', out_shape=(jax.ShapeDtypeS...]
    pallas_call x1, Pallas kernels: 85.1 us -> 66.5 us  [device_step(): pl.pallas_call(expert_kernel, name='experts', out_shape=(tile_shape, tile...]
where the time goes in v2:
time: 338 us
  Pallas kernels  331 us (98%)
  local copies, waits for them, and re-layouts  7.05 us (2%)
    pallas_call x1, Pallas kernels, device_step(): pl.pallas_call(scatter_kernel, name='scatter', out_shape=(jax.ShapeDtypeS...  140 us
    pallas_call x1, Pallas kernels, device_step(): pl.pallas_call(gather_kernel, name='gather', out_shape=(tile_shape, tile_...  124 us
    pallas_call x1, Pallas kernels, device_step(): pl.pallas_call(expert_kernel, name='experts', out_shape=(tile_shape, tile...  66.5 us

profile of v2, /device:TPU:0, one launch (start us, length us, event | category | flops | bytes accessed | tf_op | source)
XLA Modules:
  0.0 338.3 jit_solution(9697570110324134100)
XLA Ops:
  0.6 123.9 %gather.1 = (bf16[16,8,3,32,1536]{4,3,2,1,0:T(8,128)(2,1)}, bf16[16,8,3,32,1536]{4,3,2,1,0:T(8,128)(2,1)}, bf16[16,192,1536]{2,1,0:T(8,128)(2,1)}, f32[16,8,256]...) custom-call(bf16[192,1536]{1,0:T(8,128)(2,1)} %u_ref.3, ...), custom_call_target="tpu_custom_call" | custom-call | tf_op jit(solution)/shard_map/gather/pallas_call | solution.py:710
  124.5 1.6 copy.17
  126.1 66.5 %experts.1 = (bf16[16,8,3,32,1536]{4,3,2,1,0:T(8,128)(2,1)}, bf16[16,8,3,32,1536]{4,3,2,1,0:T(8,128)(2,1)}, f32[8,192,1536]{2,1,0:T(8,128)}, f32[8,192,1536]{2,1...) custom-call(s32[16,8]{1,0:T(8,128)} %bitcast.20, ...), custom_call_target="tpu_custom_call", output_to_operand_aliasing={{0}: (1, {}), {1}: (2, {})} | custom-call | tf_op jit(solution)/shard_map/experts/pallas_call | solution.py:729
  192.7 140.2 %scatter.1 = (bf16[192,1536]{1,0:T(8,128)(2,1)}, bf16[192,1536]{1,0:T(8,128)(2,1)}, f32[32,1536]{1,0:T(8,128)}) custom-call(bf16[16,768,1536]{2,1,0:T(8,128)(2,1)} %bitcast.12, bf16[16,768,1536]{2,1,0:T(8,128)(2,1)} %bitcast.13, bf16[16,192,1536]{2,1,0:T(8,128)(2,1)} %get-tuple-element.30.uall_ref, f32[16,8,256]{2,1,0:T(8,128)} %get-tuple-element.26.rank_ref, ...), custom_call_target="tpu_custom_call" | custom-call | tf_op jit(solution)/shard_map/scatter/pallas_call | solution.py:747
  332.9 1.9 copy.23
  334.8 1.9 copy.24
  336.7 1.6 copy.25

commit v3 on v2

--- a/solution.py
+++ b/solution.py
@@ -12,6 +12,7 @@
 LEVEL_ROWS = 32
 HALF = 8
 CHUNK = 512
+TAIL = 16
 
 
 def dot_nn(a, b):
@@ -79,7 +80,7 @@
 
 
 def gather_kernel(u_ref, dy_ref, ids_ref, wr_ref, x_ref, d_ref, uall_ref, rank_ref, g_ref, prob_ref, gown_ref, cnt_ref,
-                  rcv, pbuf, xbuf, in_sem, send_sem, recv_sem, meta_send, meta_recv, out_sem, uout_sem):
+                  rcv, pbuf, xbuf, in_sem, send_sem, recv_sem, tail_recv, meta_send, meta_recv, out_sem, uout_sem):
     y, c, z = position()
     me = block_of(y, c, z)
     tok = u_ref.shape[0]
@@ -114,6 +115,23 @@
 
     def send_sib(arr, s):
         return rdma(arr, s, 3, ep_sib, z)
+
+    def part(arr, s, kind, ep_to, z_to, rows, sem):
+        return pltpu.make_async_remote_copy(
+            src_ref=rcv.at[arr, s, rows], dst_ref=rcv.at[arr, s, rows], send_sem=send_sem.at[arr, s, kind],
+            recv_sem=sem.at[arr, s], device_id={"ep": ep_to, "etp": z_to}, device_id_type=MESH)
+
+    head = pl.ds(0, tok - TAIL)
+    tail = pl.ds(tok - TAIL, TAIL)
+
+    def head_y(arr, s):
+        return part(arr, s, 2, ep_y, z, head, recv_sem)
+
+    def tail_down(arr, s):
+        return part(arr, s, 0, ep_me, jnp.maximum(z - 1, 0), tail, tail_recv)
+
+    def tail_up(arr, s):
+        return part(arr, s, 1, ep_me, jnp.minimum(z + 1, 3), tail, tail_recv)
 
     for arr, own in ((0, own_u), (1, own_d)):
         own.wait()
@@ -167,47 +185,67 @@
     def u_copy(s):
         return pltpu.make_async_copy(rcv.at[0, s], uall_ref.at[s], uout_sem.at[s])
 
-    @pl.loop(0, 5)
+    @pl.loop(0, 9)
     def _(t):
-        for arr in (0, 1):
-            @pl.when((t >= 1) & (t <= 3))
-            def _():
-                zb = near_order(z, t)
-                s = block_of(y, c, zb)
-                send_y(arr, s).wait_recv()
-
-                @pl.when((zb < z) & (z < 3))
-                def _():
-                    send_up(arr, s).start()
-
-                @pl.when((zb > z) & (z > 0))
-                def _():
-                    send_down(arr, s).start()
-
-                send_y(arr, s).start()
-                send_sib(arr, s).start()
-
-        for arr in (0, 1):
-            @pl.when(t >= 1)
-            def _():
-                s = block_of(1 - y, c, near_order(z, t - 1))
-                send_y(arr, s).wait_recv()
-                send_sib(arr, s).start()
-
-        lo = 4 * (t // 4)
-        hi = jnp.where(t == 0, 4, 8)
-
-        @pl.loop(lo, hi)
+        turn = jnp.maximum(t - 1, 0)
+        arr_t = turn % 2
+        q_col = 1 + turn // 2
+        q_y = turn // 2
+
+        @pl.when((t >= 1) & (t <= 6))
+        def _():
+            zb = near_order(z, q_col)
+            s = block_of(y, c, zb)
+            send_y(arr_t, s).wait_recv()
+
+            @pl.when((zb < z) & (z < 3))
+            def _():
+                send_up(arr_t, s).start()
+
+            @pl.when((zb > z) & (z > 0))
+            def _():
+                send_down(arr_t, s).start()
+
+            head_y(arr_t, s).start()
+            send_sib(arr_t, s).start()
+
+        @pl.when(t >= 1)
+        def _():
+            zb = near_order(z, q_y)
+            s = block_of(1 - y, c, zb)
+
+            @pl.when(q_y == 0)
+            def _():
+                send_y(arr_t, s).wait_recv()
+
+            @pl.when(q_y > 0)
+            def _():
+                tail_up(arr_t, s).wait_recv()
+
+            @pl.when((zb <= z) & (z < 3))
+            def _():
+                tail_up(arr_t, s).start()
+
+            @pl.when((zb >= z) & (z > 0))
+            def _():
+                tail_down(arr_t, s).start()
+
+            @pl.when(q_y > 0)
+            def _():
+                head_y(arr_t, s).wait_recv()
+
+            send_sib(arr_t, s).start()
+
+        @pl.loop(jnp.where(t > 6, 2, 0), 4)
         def _(i):
-            typ = i // 4
-            arr = (i // 2) % 2
             flip = i % 2
+            slot = flip
+            typ = jnp.where(t == 0, 0, i // 2)
+            arr = jnp.where(t == 0, i // 2, arr_t)
             core = c + flip - 2 * c * flip
-            zb = near_order(z, t - typ)
+            zb = near_order(z, jnp.where(t == 0, 0, jnp.where(typ == 0, q_col, q_y)))
             yb = y + typ - 2 * y * typ
             s = block_of(yb, core, zb)
-            j = jnp.maximum(8 * t - 4, 0) + i - lo
-            slot = j % 2
 
             @pl.when(flip == 1)
             def _():
@@ -224,12 +262,13 @@
                 mask = g_ref[s] >= 0.0
                 ones = jnp.where(mask, 1.0, 0.0)
                 rank = dot_nn(ones.astype(BF16), before)
-                cnt_ref[s] = jnp.broadcast_to(jnp.sum(ones, axis=1, keepdims=True), cnt_ref.shape[1:]).astype(jnp.int32)
+                held = dot_nt(jnp.ones(ones.shape, BF16), ones.astype(BF16))
+                cnt_ref[pl.ds(s, 1), 0:local] = held[0:1, :].astype(jnp.int32)
                 rank_ref[s] = jnp.where(mask, rank, -1.0)
 
             pbuf[...] = one_hot_slots(rank_ref[s][:, 0:tok], cap)
 
-            @pl.when(j >= 2)
+            @pl.when((t > 0) | (i >= 2))
             def _():
                 out_copy(False, slot, s).wait()
 
@@ -266,12 +305,21 @@
             @pl.when((z > 0) & (zb >= z))
             def _():
                 send_down(arr, s).wait_send()
+                tail_down(arr, sy).wait_send()
 
             @pl.when((z < 3) & (zb <= z))
             def _():
                 send_up(arr, s).wait_send()
-
-            send_y(arr, s).wait_send()
+                tail_up(arr, sy).wait_send()
+
+            @pl.when(q == 0)
+            def _():
+                send_y(arr, s).wait_send()
+
+            @pl.when(q > 0)
+            def _():
+                head_y(arr, s).wait_send()
+
             send_sib(arr, s).wait_send()
             send_sib(arr, sy).wait_send()
 
@@ -517,12 +565,14 @@
             device_id={"ep": ep_me, "etp": z_to}, device_id_type=MESH)
 
     def plan(n):
-        arr = jnp.where(n < 12, 0, jnp.where(n < 20, 1, jnp.where(n < 24, 0, 1)))
-        phase = jnp.where(n < 8, 1, jnp.where(n < 12, 2, jnp.where(n < 20, 1, jnp.where(n < 24, 3, jnp.where(n < 28, 2, 3)))))
-        off = jnp.where(n < 8, n, n % 4)
-        off = jnp.where((n >= 12) & (n < 20), n - 12, off)
-        k = jnp.where(phase == 1, off // 2, off)
-        to_sib = jnp.where(phase == 1, 1 - off % 2, jnp.where(phase == 2, 1, 0))
+        group = (n - 12) // 3
+        rest = (n - 12) % 3
+        mid = (n >= 12) & (n < 21)
+        arr = jnp.where((n < 12) | (n == 23) | (mid & (rest == 0)), 0, 1)
+        phase = jnp.where(n < 8, 1, jnp.where(n < 12, 2, jnp.where(n < 21, jnp.where(rest == 0, 3, 1), jnp.where(n < 23, 1, jnp.where(n == 23, 3, jnp.where(n < 28, 2, 3))))))
+        sub = jnp.where(n < 8, n % 2, jnp.where(n < 21, rest - 1, n - 21))
+        k = jnp.where(n < 8, n // 2, jnp.where(n < 12, n - 8, jnp.where(n < 21, group, jnp.where(n < 24, 3, n % 4))))
+        to_sib = jnp.where(phase == 1, 1 - sub, jnp.where(phase == 2, 1, 0))
         other = jnp.where(phase == 1, 1, 0)
         core = c + to_sib - 2 * c * to_sib
         col = y + other - 2 * y * other
@@ -567,6 +617,59 @@
         def _(m):
             cols = pl.ds(pl.multiple_of(m * CHUNK, CHUNK), CHUNK)
             acc[:, cols] = dot_nn(pbuf[...], slots[slot, :, cols])
+
+        @pl.when(to_sib == 1)
+        def _():
+            idx = k + 4 * (phase - 1)
+            out = idx % 2
+
+            @pl.when((idx >= 2) | (arr == 1))
+            def _():
+                sib_copy(out, arr, idx).wait_send()
+
+            sib_out[out] = acc[...].astype(BF16)
+            sib_copy(out, arr, idx).start()
+
+        @pl.when((phase == 1) & (to_sib == 0))
+        def _():
+            sib_copy(0, arr, k).wait_recv()
+            y_out[arr, k] = (acc[...] + sib_in[arr, k].astype(F32)).astype(BF16)
+            y_copy(arr, k).start()
+
+        @pl.when(phase == 3)
+        def _():
+            sib_copy(0, arr, k + 4).wait_recv()
+            y_copy(arr, k).wait_recv()
+            acc[...] = acc[...] + sib_in[arr, k + 4].astype(F32) + y_in[arr, k].astype(F32)
+            target = far_order(z, k)
+
+            @pl.when(((target > z) & (z > 0)) | ((target < z) & (z < 3)) | ((target == z) & (z > 0)))
+            def _():
+                z_copy(arr, 0, target, z).wait_recv()
+                acc[...] += z_in[arr, target].astype(F32)
+
+            @pl.when((target == z) & (z < 3))
+            def _():
+                z_copy(arr, 0, 4, z).wait_recv()
+                acc[...] += z_in[arr, 4].astype(F32)
+
+            @pl.when(k < 3)
+            def _():
+                z_out[arr, k] = acc[...].astype(BF16)
+                z_to = jnp.where(target > z, z + 1, z - 1)
+                dst = jnp.where(target == z - 1, 4, target)
+                z_copy(arr, k, dst, z_to).start()
+
+            @pl.when((k == 3) & (arr == 0))
+            def _():
+                yo_ref[...] = (u_ref[...].astype(F32) + acc[...]).astype(BF16)
+
+            @pl.when((k == 3) & (arr == 1))
+            def _():
+                dl3 = split3(dl_all[me][:, 0:tok])
+                wr = wr_ref[...]
+                router = dot_tn(dl3, jnp.concatenate([wr, wr, wr], axis=0))
+                du_ref[...] = (dy_ref[...].astype(F32) + acc[...] + router).astype(BF16)
 
         @pl.when(n == 1)
         def _():
@@ -585,66 +688,13 @@
             def _(b):
                 dl_copy((me + b) % blocks, me).start()
 
-        @pl.when(to_sib == 1)
-        def _():
-            idx = k + 4 * (phase - 1)
-            out = idx % 2
-
-            @pl.when((idx >= 2) | (arr == 1))
-            def _():
-                sib_copy(out, arr, idx).wait_send()
-
-            sib_out[out] = acc[...].astype(BF16)
-            sib_copy(out, arr, idx).start()
-
-        @pl.when((phase == 1) & (to_sib == 0))
-        def _():
-            sib_copy(0, arr, k).wait_recv()
-            y_out[arr, k] = (acc[...] + sib_in[arr, k].astype(F32)).astype(BF16)
-            y_copy(arr, k).start()
-
-        @pl.when(phase == 3)
-        def _():
-            sib_copy(0, arr, k + 4).wait_recv()
-            y_copy(arr, k).wait_recv()
-            acc[...] = acc[...] + sib_in[arr, k + 4].astype(F32) + y_in[arr, k].astype(F32)
-            target = far_order(z, k)
-
-            @pl.when(((target > z) & (z > 0)) | ((target < z) & (z < 3)) | ((target == z) & (z > 0)))
-            def _():
-                z_copy(arr, 0, target, z).wait_recv()
-                acc[...] += z_in[arr, target].astype(F32)
-
-            @pl.when((target == z) & (z < 3))
-            def _():
-                z_copy(arr, 0, 4, z).wait_recv()
-                acc[...] += z_in[arr, 4].astype(F32)
-
-            @pl.when(k < 3)
-            def _():
-                z_out[arr, k] = acc[...].astype(BF16)
-                z_to = jnp.where(target > z, z + 1, z - 1)
-                dst = jnp.where(target == z - 1, 4, target)
-                z_copy(arr, k, dst, z_to).start()
-
-            @pl.when((k == 3) & (arr == 0))
-            def _():
-                yo_ref[...] = (u_ref[...].astype(F32) + acc[...]).astype(BF16)
-
-            @pl.when((k == 3) & (arr == 1))
-            def _():
-                dl3 = split3(dl_all[me][:, 0:tok])
-                wr = wr_ref[...]
-                router = dot_tn(dl3, jnp.concatenate([wr, wr, wr], axis=0))
-                du_ref[...] = (dy_ref[...].astype(F32) + acc[...] + router).astype(BF16)
-
-        @pl.when((n >= 11) & (n < 27))
-        def _():
-            u_load(n - 11).start()
-
-        @pl.when((n >= 12) & (n < 28))
-        def _():
-            b = n - 12
+        @pl.when((n >= 15) & (n < 31))
+        def _():
+            u_load(n - 15).start()
+
+        @pl.when(n >= 16)
+        def _():
+            b = n - 16
 
             @pl.when(b != me)
             def _():
@@ -711,14 +761,14 @@
             gather_kernel,
             name="gather",
             out_shape=(tile_shape, tile_shape, jax.ShapeDtypeStruct((blocks, tok, d_model), BF16), meta_shape, meta_shape, own_shape, own_shape,
-                       jax.ShapeDtypeStruct((blocks, local, 128), jnp.int32)),
+                       jax.ShapeDtypeStruct((blocks, 128), jnp.int32)),
             in_specs=[any_spec, any_spec, vmem, vmem],
             out_specs=(any_spec, any_spec, any_spec, vmem, vmem, vmem, vmem, vmem),
             scratch_shapes=[
                 pltpu.VMEM((2, blocks, tok, d_model), BF16),
                 pltpu.VMEM((slots, tok), BF16),
                 pltpu.VMEM((2, local, levels, LEVEL_ROWS, d_model), BF16),
-                dma((2,)), dma((2, blocks, 4)), dma((2, blocks)), dma((blocks,)), dma((blocks,)), dma((2,)), dma((blocks,)),
+                dma((2,)), dma((2, blocks, 4)), dma((2, blocks)), dma((2, blocks)), dma((blocks,)), dma((blocks,)), dma((2,)), dma((blocks,)),
             ],
             compiler_params=pltpu.CompilerParams(has_side_effects=True, vmem_limit_bytes=60 * 1024 * 1024),
         )(u_loc, dy_loc, ids_t, wr_t)
@@ -741,7 +791,7 @@
             ],
             input_output_aliases={1: 0, 2: 1},
             compiler_params=pltpu.CompilerParams(vmem_limit_bytes=60 * 1024 * 1024),
-        )(counts[:, :, 0], x_slots, d_slots, wg_t, wu_t, w_down, rank, gate)
+        )(counts, x_slots, d_slots, wg_t, wu_t, w_down, rank, gate)
 
         slot_shape = (blocks, slots, d_model)
         y_loc, du_loc, dwr_t = pl.pallas_call(

time: 338 us -> 328 us (0.970)
  Pallas kernels: 331 us -> 321 us
    pallas_call x1, Pallas kernels: 140 us -> 129 us  [device_step(): pl.pallas_call(scatter_kernel, name='scatter', out_shape=(jax.ShapeDtypeS...]
where the time goes in v3:
time: 328 us; the launch traced here: 327 us
  Pallas kernels  321 us (98%)
  local copies, waits for them, and re-layouts  5.45 us (2%)
    pallas_call x1, Pallas kernels, device_step(): pl.pallas_call(scatter_kernel, name='scatter', out_shape=(jax.ShapeDtypeS...  129 us
    pallas_call x1, Pallas kernels, device_step(): pl.pallas_call(gather_kernel, name='gather', out_shape=(tile_shape, tile_...  123 us
    pallas_call x1, Pallas kernels, device_step(): pl.pallas_call(expert_kernel, name='experts', out_shape=(tile_shape, tile...  69.7 us

profile of v3, /device:TPU:0, one launch (start us, length us, event | category | flops | bytes accessed | tf_op | source)
XLA Modules:
  0.0 327.4 jit_solution(16428540956280599607)
XLA Ops:
  0.6 122.9 %gather.1 = (bf16[16,8,3,32,1536]{4,3,2,1,0:T(8,128)(2,1)}, bf16[16,8,3,32,1536]{4,3,2,1,0:T(8,128)(2,1)}, bf16[16,192,1536]{2,1,0:T(8,128)(2,1)}, f32[16,8,256]...) custom-call(bf16[192,1536]{1,0:T(8,128)(2,1)} %u_ref.3, ...), custom_call_target="tpu_custom_call" | custom-call | tf_op jit(solution)/shard_map/gather/pallas_call | solution.py:760
  123.6 69.7 %experts.1 = (bf16[16,8,3,32,1536]{4,3,2,1,0:T(8,128)(2,1)}, bf16[16,8,3,32,1536]{4,3,2,1,0:T(8,128)(2,1)}, f32[8,192,1536]{2,1,0:T(8,128)}, f32[8,192,1536]{2,1...) custom-call(s32[16,128]{1,0:T(8,128)} %get-tuple-element.23.cnt, ...), custom_call_target="tpu_custom_call", output_to_operand_aliasing={{0}: (1, {}), {1}: (2, {})} | custom-call | tf_op jit(solution)/shard_map/experts/pallas_call | solution.py:779
  193.3 128.6 %scatter.1 = (bf16[192,1536]{1,0:T(8,128)(2,1)}, bf16[192,1536]{1,0:T(8,128)(2,1)}, f32[32,1536]{1,0:T(8,128)}) custom-call(bf16[16,768,1536]{2,1,0:T(8,128)(2,1)} %bitcast.9, bf16[16,768,1536]{2,1,0:T(8,128)(2,1)} %bitcast.10, bf16[16,192,1536]{2,1,0:T(8,128)(2,1)} %get-tuple-element.30.uall_ref, f32[16,8,256]{2,1,0:T(8,128)} %get-tuple-element.26.rank_ref, ...), custom_call_target="tpu_custom_call" | custom-call | tf_op jit(solution)/shard_map/scatter/pallas_call | solution.py:797
  322.0 1.9 copy.20
  323.9 1.9 copy.21
  325.8 1.6 copy.22

commit v4 on v3

--- a/solution.py
+++ b/solution.py
@@ -12,7 +12,10 @@
 LEVEL_ROWS = 32
 HALF = 8
 CHUNK = 512
+EXPERT_CHUNK = 256
 TAIL = 16
+PAIR = (0, 1)
+VMEM_LIMIT = 60 * 1024 * 1024
 
 
 def dot_nn(a, b):
@@ -33,8 +36,28 @@
     return ep // 2, ep % 2, z
 
 
+def flipped(a):
+    return 1 - a
+
+
+def swap(a, b):
+    return a + b - 2 * a * b
+
+
+def ep_of(y, c):
+    return y * 2 + c
+
+
+def device_of(s):
+    return {"ep": s // 4, "etp": s % 4}
+
+
+def as_one(hit):
+    return jnp.where(hit, 1.0, 0.0)
+
+
 def block_of(y, c, z):
-    return (y * 2 + c) * 4 + z
+    return ep_of(y, c) * 4 + z
 
 
 def near_order(z, q):
@@ -56,7 +79,7 @@
     experts = rank.shape[0]
     row = lax.broadcasted_iota(jnp.int32, (experts, cap, tok), 1).astype(F32)
     hit = rank[:, None, :] == row
-    return jnp.where(hit, 1.0, 0.0).reshape(experts * cap, tok).astype(BF16)
+    return as_one(hit).reshape(experts * cap, tok).astype(BF16)
 
 
 def one_hot_tokens(rank, cap):
@@ -64,11 +87,11 @@
     lane = lax.broadcasted_iota(jnp.int32, (experts, experts * cap), 1)
     first = lax.broadcasted_iota(jnp.int32, (experts, experts * cap), 0) * cap
     mine = (lane >= first) & (lane < first + cap)
-    spread = dot_tn(rank.astype(BF16), jnp.where(mine, 1.0, 0.0).astype(BF16))
+    spread = dot_tn(rank.astype(BF16), as_one(mine).astype(BF16))
     row = lax.broadcasted_iota(jnp.int32, (1, experts * cap), 1)
     for e in range(1, experts):
         row = row - jnp.where(lane[0:1] >= e * cap, cap, 0)
-    return jnp.where(spread == row.astype(F32), 1.0, 0.0).astype(BF16)
+    return as_one(spread == row.astype(F32)).astype(BF16)
 
 
 def split3(x):
@@ -100,9 +123,9 @@
             src_ref=rcv.at[arr, s], dst_ref=rcv.at[arr, s], send_sem=send_sem.at[arr, s, kind],
             recv_sem=recv_sem.at[arr, s], device_id={"ep": ep_to, "etp": z_to}, device_id_type=MESH)
 
-    ep_sib = y * 2 + 1 - c
-    ep_y = (1 - y) * 2 + c
-    ep_me = y * 2 + c
+    ep_sib = ep_of(y, flipped(c))
+    ep_y = ep_of(flipped(y), c)
+    ep_me = ep_of(y, c)
 
     def send_down(arr, s):
         return rdma(arr, s, 0, ep_me, jnp.maximum(z - 1, 0))
@@ -164,7 +187,7 @@
         ep_to = s // 4
         return pltpu.make_async_remote_copy(
             src_ref=gown_ref.at[pl.ds(pl.multiple_of(ep_to * local, local), local), :], dst_ref=g_ref.at[me],
-            send_sem=meta_send.at[s], recv_sem=meta_recv.at[me], device_id={"ep": ep_to, "etp": s % 4},
+            send_sem=meta_send.at[s], recv_sem=meta_recv.at[me], device_id=device_of(s),
             device_id_type=MESH)
 
     def meta_wait(s):
@@ -177,7 +200,7 @@
         meta_copy((me + i) % blocks).start()
 
     lower = (lax.broadcasted_iota(jnp.int32, (LANES, LANES), 0) < lax.broadcasted_iota(jnp.int32, (LANES, LANES), 1))
-    before = jnp.where(lower, 1.0, 0.0).astype(BF16)
+    before = as_one(lower).astype(BF16)
 
     def out_copy(arr_is_dy, slot, s):
         return pltpu.make_async_copy(xbuf.at[slot], (d_ref if arr_is_dy else x_ref).at[s], out_sem.at[slot])
@@ -212,7 +235,7 @@
         @pl.when(t >= 1)
         def _():
             zb = near_order(z, q_y)
-            s = block_of(1 - y, c, zb)
+            s = block_of(flipped(y), c, zb)
 
             @pl.when(q_y == 0)
             def _():
@@ -242,9 +265,9 @@
             slot = flip
             typ = jnp.where(t == 0, 0, i // 2)
             arr = jnp.where(t == 0, i // 2, arr_t)
-            core = c + flip - 2 * c * flip
+            core = swap(c, flip)
             zb = near_order(z, jnp.where(t == 0, 0, jnp.where(typ == 0, q_col, q_y)))
-            yb = y + typ - 2 * y * typ
+            yb = swap(y, typ)
             s = block_of(yb, core, zb)
 
             @pl.when(flip == 1)
@@ -260,7 +283,7 @@
                     meta_wait(s).wait_recv()
 
                 mask = g_ref[s] >= 0.0
-                ones = jnp.where(mask, 1.0, 0.0)
+                ones = as_one(mask)
                 rank = dot_nn(ones.astype(BF16), before)
                 held = dot_nt(jnp.ones(ones.shape, BF16), ones.astype(BF16))
                 cnt_ref[pl.ds(s, 1), 0:local] = held[0:1, :].astype(jnp.int32)
@@ -285,7 +308,7 @@
             def _():
                 out_copy(True, slot, s).start()
 
-    for slot in (0, 1):
+    for slot in PAIR:
         out_copy(False, slot, me).wait()
 
     @pl.loop(0, blocks)
@@ -300,8 +323,8 @@
     def _(q):
         zb = near_order(z, q)
         s = block_of(y, c, zb)
-        sy = block_of(1 - y, c, zb)
-        for arr in (0, 1):
+        sy = block_of(flipped(y), c, zb)
+        for arr in PAIR:
             @pl.when((z > 0) & (zb >= z))
             def _():
                 send_down(arr, s).wait_send()
@@ -380,14 +403,14 @@
         sig = jax.nn.sigmoid(h1)
         silu = h1 * sig
         act = (silu * h3).astype(BF16)
-        chunks = [slice(n, n + CHUNK) for n in range(0, d_model, CHUNK)]
+        chunks = [slice(n, n + EXPERT_CHUNK) for n in range(0, d_model, EXPERT_CHUNK)]
         dg = jnp.zeros((rows, 1), F32)
         da = jnp.zeros((rows, act.shape[1]), F32)
         for cols in chunks:
             out = dot_nn(act, self.wb[p, 2, :, cols])
-            dy = self.db[slot, :, :, cols].reshape(rows, CHUNK).astype(F32)
+            dy = self.db[slot, :, :, cols].reshape(rows, EXPERT_CHUNK).astype(F32)
             dg = dg + jnp.sum(out * dy, axis=1, keepdims=True)
-            self.gob[slot, :, :, cols] = (out * g_slot).astype(BF16).reshape(HALF, LEVEL_ROWS, CHUNK)
+            self.gob[slot, :, :, cols] = (out * g_slot).astype(BF16).reshape(HALF, LEVEL_ROWS, EXPERT_CHUNK)
             do = (dy * g_slot).astype(BF16)
             dob[:, cols] = do
             da = da + dot_nt(do, self.wb[p, 2, :, cols])
@@ -396,14 +419,14 @@
         dh3 = (da * silu).astype(BF16)
         for cols in chunks:
             dx = dot_nn(dh1, self.wb[p, 0, :, cols]) + dot_nn(dh3, self.wb[p, 1, :, cols])
-            self.dxb[slot, :, :, cols] = dx.astype(BF16).reshape(HALF, LEVEL_ROWS, CHUNK)
+            self.dxb[slot, :, :, cols] = dx.astype(BF16).reshape(HALF, LEVEL_ROWS, EXPERT_CHUNK)
         sgb[0] = jnp.sum(jnp.where(hit, dg.reshape(HALF, LEVEL_ROWS, 1), 0.0), axis=1)
         for j in range(HALF):
             dg_ref[self.sg[i * HALF + j] // 4, one, :] += sgb[0, pl.ds(j, 1), :]
 
         def add_dw(first):
             for cols in chunks:
-                xc = self.xb[slot, :, :, cols].reshape(rows, CHUNK)
+                xc = self.xb[slot, :, :, cols].reshape(rows, EXPERT_CHUNK)
                 for j, (left, right) in enumerate(((dh1, xc), (dh3, xc), (act, dob[:, cols]))):
                     part = dot_tn(left, right)
                     dwb[p, j, :, cols] = part if first else dwb[p, j, :, cols] + part
@@ -484,13 +507,13 @@
 
         @pl.when(i + 1 < count)
         def _():
-            tiles.load(i + 1, 1 - slot, start)
+            tiles.load(i + 1, flipped(slot), start)
 
         @pl.when(fresh)
         def _():
             @pl.when(e + 1 < local)
             def _():
-                for copy in tiles.weights(e + 1, 1 - p):
+                for copy in tiles.weights(e + 1, flipped(p)):
                     copy.start()
 
             for copy in tiles.weights(e, p):
@@ -518,7 +541,7 @@
         return carry
 
     lax.fori_loop(0, count, step, 0)
-    for p in (0, 1):
+    for p in PAIR:
         i = count - 2 + p
         tiles.store(i, i % 2, wait)
         for copy in dw_out(0, p):
@@ -531,9 +554,9 @@
                    ld_sem, sib_ss, sib_rs, y_ss, y_rs, z_ss, z_rs, dg_ss, dg_rs, dl_ss, dl_rs, u_sem):
     y, c, z = position()
     me = block_of(y, c, z)
-    ep_me = y * 2 + c
-    ep_sib = y * 2 + 1 - c
-    ep_y = (1 - y) * 2 + c
+    ep_me = ep_of(y, c)
+    ep_sib = ep_of(y, flipped(c))
+    ep_y = ep_of(flipped(y), c)
     blocks, local, lanes = rank_ref.shape
     tok, d_model = u_ref.shape
     cap = pbuf.shape[1] // local
@@ -542,12 +565,12 @@
     def dg_copy(s, src):
         return pltpu.make_async_remote_copy(
             src_ref=dgb_ref.at[s], dst_ref=dg_in.at[src], send_sem=dg_ss.at[s], recv_sem=dg_rs.at[src],
-            device_id={"ep": s // 4, "etp": s % 4}, device_id_type=MESH)
+            device_id=device_of(s), device_id_type=MESH)
 
     def dl_copy(s, src):
         return pltpu.make_async_remote_copy(
             src_ref=dl_all.at[src], dst_ref=dl_all.at[src], send_sem=dl_ss.at[s], recv_sem=dl_rs.at[src],
-            device_id={"ep": s // 4, "etp": s % 4}, device_id_type=MESH)
+            device_id=device_of(s), device_id_type=MESH)
 
     def sib_copy(slot, arr, k):
         return pltpu.make_async_remote_copy(
@@ -574,8 +597,8 @@
         k = jnp.where(n < 8, n // 2, jnp.where(n < 12, n - 8, jnp.where(n < 21, group, jnp.where(n < 24, 3, n % 4))))
         to_sib = jnp.where(phase == 1, 1 - sub, jnp.where(phase == 2, 1, 0))
         other = jnp.where(phase == 1, 1, 0)
-        core = c + to_sib - 2 * c * to_sib
-        col = y + other - 2 * y * other
+        core = swap(c, to_sib)
+        col = swap(y, other)
         return arr, phase, k, to_sib, block_of(col, core, far_order(z, k))
 
     def start_load(n, slot):
@@ -608,7 +631,7 @@
 
         @pl.when(n < 31)
         def _():
-            start_load(n + 1, 1 - slot)
+            start_load(n + 1, flipped(slot))
 
         pbuf[...] = one_hot_tokens(rank_ref[s][:, 0:tok], cap)
         pltpu.make_async_copy(go_ref.at[s], slots.at[slot], ld_sem.at[slot]).wait()
@@ -704,12 +727,12 @@
             part = dot_nn(split3(dl_all[b][:, 0:tok]), ubuf[b % 2])
             dwr_ref[...] += part[0:experts] + part[experts:2 * experts] + part[2 * experts:3 * experts]
 
-    for out in (0, 1):
+    for out in PAIR:
         sib_copy(out, 0, 0).wait_send()
 
     @pl.loop(0, 4)
     def _(k):
-        for arr in (0, 1):
+        for arr in PAIR:
             y_copy(arr, k).wait_send()
 
             @pl.when(k < 3)
@@ -770,7 +793,7 @@
                 pltpu.VMEM((2, local, levels, LEVEL_ROWS, d_model), BF16),
                 dma((2,)), dma((2, blocks, 4)), dma((2, blocks)), dma((2, blocks)), dma((blocks,)), dma((blocks,)), dma((2,)), dma((blocks,)),
             ],
-            compiler_params=pltpu.CompilerParams(has_side_effects=True, vmem_limit_bytes=60 * 1024 * 1024),
+            compiler_params=pltpu.CompilerParams(has_side_effects=True, vmem_limit_bytes=VMEM_LIMIT),
         )(u_loc, dy_loc, ids_t, wr_t)
 
         max_tiles = local * levels * (blocks // HALF) + 8
@@ -790,7 +813,7 @@
                 dma((2, 2, HALF + 1)), dma((2, 2, HALF + 1)), dma((2, 3)), dma((2, 3)),
             ],
             input_output_aliases={1: 0, 2: 1},
-            compiler_params=pltpu.CompilerParams(vmem_limit_bytes=60 * 1024 * 1024),
+            compiler_params=pltpu.CompilerParams(vmem_limit_bytes=VMEM_LIMIT),
         )(counts, x_slots, d_slots, wg_t, wu_t, w_down, rank, gate)
 
         slot_shape = (blocks, slots, d_model)
@@ -816,7 +839,7 @@
                 dma((2,)), dma((2,)), dma((2, 8)), dma((2, 4)), dma((2, 4)), dma((2, 3)), dma((2, 5)),
                 dma((blocks,)), dma((blocks,)), dma((blocks,)), dma((blocks,)), dma((2,)),
             ],
-            compiler_params=pltpu.CompilerParams(has_side_effects=True, vmem_limit_bytes=60 * 1024 * 1024),
+            compiler_params=pltpu.CompilerParams(has_side_effects=True, vmem_limit_bytes=VMEM_LIMIT),
         )(go.reshape(slot_shape), dx.reshape(slot_shape), u_all, rank, dg_blocks, prob, g_own, u_loc, dy_loc, wr_t)
 
         dw_gate = jnp.swapaxes(dwg, 1, 2)

time: 328 us -> 325 us (level)
  no operation moved by 1% of the time
where the time goes in v4:
time: 325 us
  Pallas kernels  319 us (98%)
  local copies, waits for them, and re-layouts  5.45 us (2%)
    pallas_call x1, Pallas kernels, device_step(): pl.pallas_call(scatter_kernel, name='scatter', out_shape=(jax.ShapeDtypeS...  125 us
    pallas_call x1, Pallas kernels, device_step(): pl.pallas_call(gather_kernel, name='gather', out_shape=(tile_shape, tile_...  123 us
    pallas_call x1, Pallas kernels, device_step(): pl.pallas_call(expert_kernel, name='experts', out_shape=(tile_shape, tile...  70.5 us

profile of v4, /device:TPU:0, one launch (start us, length us, event | category | flops | bytes accessed | tf_op | source)
XLA Modules:
  0.0 324.9 jit_solution(1814273792782420782)
XLA Ops:
  0.6 122.9 %gather.1 = (bf16[16,8,3,32,1536]{4,3,2,1,0:T(8,128)(2,1)}, bf16[16,8,3,32,1536]{4,3,2,1,0:T(8,128)(2,1)}, bf16[16,192,1536]{2,1,0:T(8,128)(2,1)}, f32[16,8,256]...) custom-call(bf16[192,1536]{1,0:T(8,128)(2,1)} %u_ref.3, ...), custom_call_target="tpu_custom_call" | custom-call | tf_op jit(solution)/shard_map/gather/pallas_call | solution.py:783
  123.6 70.5 %experts.1 = (bf16[16,8,3,32,1536]{4,3,2,1,0:T(8,128)(2,1)}, bf16[16,8,3,32,1536]{4,3,2,1,0:T(8,128)(2,1)}, f32[8,192,1536]{2,1,0:T(8,128)}, f32[8,192,1536]{2,1...) custom-call(s32[16,128]{1,0:T(8,128)} %get-tuple-element.23.cnt, ...), custom_call_target="tpu_custom_call", output_to_operand_aliasing={{0}: (1, {}), {1}: (2, {})} | custom-call | tf_op jit(solution)/shard_map/experts/pallas_call | solution.py:802
  194.1 125.4 %scatter.1 = (bf16[192,1536]{1,0:T(8,128)(2,1)}, bf16[192,1536]{1,0:T(8,128)(2,1)}, f32[32,1536]{1,0:T(8,128)}) custom-call(bf16[16,768,1536]{2,1,0:T(8,128)(2,1)} %bitcast.9, bf16[16,768,1536]{2,1,0:T(8,128)(2,1)} %bitcast.10, bf16[16,192,1536]{2,1,0:T(8,128)(2,1)} %get-tuple-element.30.uall_ref, f32[16,8,256]{2,1,0:T(8,128)} %get-tuple-element.26.rank_ref, ...), custom_call_target="tpu_custom_call" | custom-call | tf_op jit(solution)/shard_map/scatter/pallas_call | solution.py:820
  319.4 1.9 copy.20
  321.4 1.9 copy.21
  323.3 1.6 copy.22
